TPU v7x, 256 devices: a whole 4x4x8 slice. The times are simulated.
256 devices in a mesh: dp: 16 (over x_lo, y, core), expert: 16 (over x_hi, z).
Axes of the slice: x: 4 (x_hi: 2, x_lo: 2; x = x_hi * 2 + x_lo), y: 4, z: 8, core: 2. Of those that a mesh axis runs over, the one named last changes fastest.
Arguments:
- tokens: bfloat16 [2048, 2048], P('expert', 'dp'), may hold values from -6 to 6
- routes: int32 [2048, 2], P('expert'), may hold values from 0 to 15, all different within a row
- dt_raw: float32 [2048, 32], P('expert', 'dp'), may hold values from -5 to 5
- b_proj: float32 [2048, 16], P('expert'), may hold values from -1.8 to 1.8
- c_proj: float32 [2048, 16], P('expert'), may hold values from -1.8 to 1.8
- decay_rate: float32 [32], P('dp'), may hold values from 0.002 to 0.2
- skip_gain: float32 [32], P('dp'), may hold values from 0.5 to 1.5
- router_weight: float32 [2048, 16], P('dp'), may hold values from -0.125 to 0.125
- gate_weight: bfloat16 [16, 2048, 7168], P('expert', None, 'dp'), may hold values from -0.125 to 0.125
- up_weight: bfloat16 [16, 2048, 7168], P('expert', None, 'dp'), may hold values from -0.125 to 0.125
- down_weight: bfloat16 [16, 7168, 2048], P('expert', 'dp'), may hold values from -0.0625 to 0.0625
- out_grad: bfloat16 [2048, 2048], P('expert', 'dp'), may hold values from -6 to 6
Outputs:
- block_out: bfloat16 [2048, 2048], P('expert', 'dp')
- token_grad: bfloat16 [2048, 2048], P('expert', 'dp')
- gate_grad: bfloat16 [16, 2048, 7168], P('expert', None, 'dp')
- up_grad: bfloat16 [16, 2048, 7168], P('expert', None, 'dp')
- down_grad: bfloat16 [16, 7168, 2048], P('expert', 'dp')
- router_grad: float32 [2048, 16], P('dp')
- rate_grad: float32 [32], P('dp')
- skip_grad: float32 [32], P('dp')
Inputs may be any that keep to these rules, and one draw needn't show every extreme that they name: `routes`: each token names two different experts.
All inputs are finite; a program needn't handle non-finite values.
Results may differ from a plain program's by a relative error of at most 0.02.
Values may be sent and summed in bfloat16 or wider, within the bound.
A program may use at most 64 MiB of HBM per device.

v0:
```python
import jax
import jax.numpy as jnp
from jax import lax
from jax.sharding import PartitionSpec as P

D = 2048


EPSILON = 1e-06
HIGHEST = lax.Precision.HIGHEST


def sent_to_all(x, axis):
    peers = lax.axis_size(axis)
    return lax.all_to_all(jnp.broadcast_to(x[None], (peers, *x.shape)), axis, 0, 0, tiled=True)


def taken_together(x, axis):
    return sent_to_all(x, axis).sum(axis=0)


def gathered_once(x, axis):
    leaves = jax.tree.leaves(x)
    order = sorted(range(len(leaves)), key=lambda k: -leaves[k].size)
    width = (1, *leaves[order[0]].shape)[-1]
    lines = [
        jnp.pad(leaves[k].reshape(-1), (0, -leaves[k].size % width)).reshape(-1, width)
        for k in order
    ]
    both, at, found = (sent_to_all(jnp.concatenate(lines), axis), 0, {})
    for k, line in zip(order, lines):
        slab = both[:, at : at + len(line)].reshape(len(both), -1)
        found[k] = slab[:, : leaves[k].size].reshape(-1, *leaves[k].shape)
        at += len(line)
    numbers = iter(range(len(leaves)))
    return jax.tree.map(lambda _: found[next(numbers)], x)


def once_a_type(x, axis):
    leaves, found = (jax.tree.leaves(x), {})
    for initial, a in enumerate(leaves):
        if initial not in found:
            alike = [k for k, b in enumerate(leaves) if b.dtype == a.dtype]
            got = (
                gathered_once([leaves[k] for k in alike], axis)
                if len(alike) > 1
                else [sent_to_all(a, axis)]
            )
            for k, b in zip(alike, got):
                found[k] = b
    numbers = iter(range(len(leaves)))
    return jax.tree.map(lambda _: found[next(numbers)], x)


def combined_pairwise(pieces, combine):
    while len(jax.tree.leaves(pieces)[0]) > 1:
        pieces = jax.vmap(combine)(
            *(jax.tree.map(lambda part: part[side::2], pieces) for side in (0, 1))
        )
    return jax.tree.map(lambda part: part[0], pieces)


def carried_in(x, axis, combine, identity, reverse):
    peers, place = (lax.axis_size(axis), lax.axis_index(axis))
    passed = jnp.arange(peers) > place if reverse else jnp.arange(peers) < place

    def kept(part, zero, own):
        part = jnp.where(
            passed.reshape(-1, *(1 for _ in own.shape)), part, jnp.asarray(zero, own.dtype)
        )
        return part[::-1] if reverse else part

    pieces = once_a_type(x, axis)
    return combined_pairwise(jax.tree.map(kept, pieces, identity, x), combine)


def in_order(tiles, dim):
    lengths = list(tiles.shape[1:])
    lengths[dim] *= tiles.shape[0]
    return jnp.moveaxis(tiles, 0, dim).reshape(lengths)


def gather_directly(x, axis, dim):
    tiles = sent_to_all(x, axis)
    return in_order(tiles, dim)


def split_up(x, dim, peers):
    lengths = x.shape
    tiles = x.reshape(*lengths[:dim], peers, lengths[dim] // peers, *lengths[dim + 1 :])
    return jnp.moveaxis(tiles, dim, 0)


def sent_and_summed(x, axis, dim):
    peers = lax.axis_size(axis)
    tiles = lax.all_to_all(split_up(x, dim, peers), axis, 0, 0, tiled=True)
    return jnp.sum(tiles.astype(jnp.float32), axis=0)


def in_one(arrays, axis):
    vector, at, finished = (jnp.concatenate([a.reshape(-1) for a in arrays]), 0, [])
    total = taken_together(vector, axis)
    for a in arrays:
        finished.append(total[at : at + a.size].reshape(a.shape))
        at += a.size
    return tuple(finished)


def end_parts(normed, b_rows, dt_rows, decay_rate):
    steps_total = normed.shape[0]
    head_count = decay_rate.shape[0]
    step_size = jax.nn.softplus(dt_rows)
    running = jnp.cumsum(-step_size * decay_rate[None, :], axis=0)
    tail_weight = jnp.exp(running[-1][None, :] - running) * step_size
    head_rows = normed.reshape(steps_total, head_count, -1)
    local_state = jnp.einsum("sh,shp,sn->hpn", tail_weight, head_rows, b_rows, precision=HIGHEST)
    return (jnp.exp(running[-1]), local_state.reshape(head_count, -1))


def ssd_piece(normed, b_rows, c_rows, dt_rows, decay_rate, skip_gain, state_start):
    steps_total = normed.shape[0]
    head_count = decay_rate.shape[0]
    state_width = b_rows.shape[1]
    step_size = jax.nn.softplus(dt_rows)
    running = jnp.cumsum(-step_size * decay_rate[None, :], axis=0)
    positions = jnp.arange(steps_total, dtype=jnp.int32)
    causal = (positions[:, None] >= positions[None, :])[:, :, None]
    spread = jnp.where(causal, running[:, None, :] - running[None, :, :], 0.0)
    decay_table = jnp.where(causal, jnp.exp(spread), 0.0)
    pairing = jnp.dot(c_rows, b_rows.T, precision=HIGHEST)
    mixing = decay_table * pairing[:, :, None] * step_size[None, :, :]
    head_rows = normed.reshape(steps_total, head_count, -1)
    state_three = state_start.reshape(head_count, -1, state_width)
    mixed = jnp.einsum("tsh,shp->thp", mixing, head_rows, precision=HIGHEST)
    mixed = mixed + jnp.einsum(
        "tn,th,hpn->thp", c_rows, jnp.exp(running), state_three, precision=HIGHEST
    )
    mixed = mixed + skip_gain[None, :, None] * head_rows
    decay_total, local_state = end_parts(normed, b_rows, dt_rows, decay_rate)
    state_end = decay_total[:, None] * state_start + local_state
    return (mixed.reshape(steps_total, -1), state_end)


def dispatch_table(choice_ids, expert_count, capacity):
    flat_ids = choice_ids.reshape(-1)
    row_total = flat_ids.shape[0]
    expert_hot = (flat_ids[:, None] == jnp.arange(expert_count, dtype=jnp.int32)[None, :]).astype(
        jnp.float32
    )
    positions = jnp.arange(row_total, dtype=jnp.int32)
    lower = (positions[:, None] > positions[None, :]).astype(jnp.float32)
    earlier = jnp.dot(lower, expert_hot, precision=HIGHEST)
    slot_index = jnp.sum(earlier * expert_hot, axis=1)
    target = flat_ids.astype(jnp.float32) * capacity + slot_index
    target = jnp.where(slot_index < capacity, target, -1.0)
    slot_ids = jnp.arange(expert_count * capacity, dtype=jnp.int32).astype(jnp.float32)
    return (slot_ids[:, None] == target[None, :]).astype(jnp.float32)


def feature_sum(values):
    return taken_together(values, "dp")


def norm_scale(values):
    total = feature_sum(jnp.sum(values * values, axis=-1, keepdims=True))
    return lax.rsqrt(total / D + EPSILON)


def norm_back(values, scale, grad):
    inner = feature_sum(jnp.sum(grad * values, axis=-1, keepdims=True))
    return scale * grad - values * (scale * scale * scale) * (inner / D)


def link_states(earlier, later):
    return (earlier[0] * later[0], later[0][:, None] * earlier[1] + later[1])


def carry_states(decay_total, state_part, backward):
    identity = (jnp.ones_like(decay_total), jnp.zeros_like(state_part))
    result = carried_in((decay_total, state_part), "expert", link_states, identity, backward)
    return result[1]


def to_units(send_rows):
    arrived = lax.all_to_all(send_rows, "expert", split_axis=0, concat_axis=0, tiled=True)
    flat_rows = arrived.reshape(-1, arrived.shape[2])
    return gather_directly(flat_rows, "dp", 1)


def from_units(terms, expert_count):
    summed = sent_and_summed(terms.astype(jnp.bfloat16), "dp", 1)
    shaped = summed.astype(jnp.bfloat16).reshape(expert_count, -1, summed.shape[1])
    returned = lax.all_to_all(shaped, "expert", split_axis=0, concat_axis=0, tiled=True)
    return returned.reshape(-1, summed.shape[1])


def body(
    tokens,
    routes,
    dt_raw,
    b_proj,
    c_proj,
    decay_rate,
    skip_gain,
    router_weight,
    gate_weight,
    up_weight,
    down_weight,
    out_grad,
):
    tok_count = tokens.shape[0]
    feature_count = tokens.shape[1]
    expert_count = lax.axis_size("expert")
    capacity = 5 * tok_count // (2 * expert_count)
    inputs = tokens.astype(jnp.float32)
    scale_one = norm_scale(inputs)
    normed = inputs * scale_one
    decay_total, local_state = end_parts(normed, b_proj, dt_raw, decay_rate)
    state_in = carry_states(decay_total, local_state, False)

    def mixer(normed_in, rate_in, skip_in, state_start):
        return ssd_piece(normed_in, b_proj, c_proj, dt_raw, rate_in, skip_in, state_start)

    (mixed, state_end), mixer_pull = jax.vjp(mixer, normed, decay_rate, skip_gain, state_in)
    resid = (inputs + mixed).astype(jnp.bfloat16)
    resid_f = resid.astype(jnp.float32)
    scale_two = norm_scale(resid_f)
    moe_in = (resid_f * scale_two).astype(jnp.bfloat16)
    moe_f = moe_in.astype(jnp.float32)
    logits = feature_sum(jnp.dot(moe_f, router_weight, precision=HIGHEST))
    expert_ids = jnp.arange(expert_count, dtype=jnp.int32)
    first_hot = (routes[:, 0:1] == expert_ids[None, :]).astype(jnp.float32)
    second_hot = (routes[:, 1:2] == expert_ids[None, :]).astype(jnp.float32)
    logit_gap = jnp.sum(logits * (first_hot - second_hot), axis=1)
    first_weight = jax.nn.sigmoid(logit_gap)
    second_weight = jax.nn.sigmoid(-logit_gap)
    table_b = dispatch_table(routes, expert_count, capacity).astype(jnp.bfloat16)
    doubled = jnp.repeat(moe_in, 2, axis=0)
    send_rows = jnp.dot(table_b, doubled, preferred_element_type=jnp.float32).astype(jnp.bfloat16)
    unit_rows = to_units(send_rows.reshape(expert_count, capacity, feature_count))
    gate_pre = jnp.dot(unit_rows, gate_weight[0], preferred_element_type=jnp.float32)
    up_pre = jnp.dot(unit_rows, up_weight[0], preferred_element_type=jnp.float32)
    hidden = (jax.nn.silu(gate_pre) * up_pre).astype(jnp.bfloat16)
    down_terms = jnp.dot(hidden, down_weight[0], preferred_element_type=jnp.float32)
    back_rows = from_units(down_terms, expert_count)
    per_slot = lax.dot_general(
        table_b, back_rows, (((0,), (0,)), ((), ())), preferred_element_type=jnp.float32
    )
    per_slot = per_slot.reshape(tok_count, 2, feature_count)
    moe_sum = first_weight[:, None] * per_slot[:, 0] + second_weight[:, None] * per_slot[:, 1]
    block_out = (resid_f + moe_sum).astype(jnp.bfloat16)
    upstream = out_grad.astype(jnp.float32)
    back_pair = feature_sum(jnp.sum(upstream[:, None, :] * per_slot, axis=2))
    first_back = back_pair[:, 0]
    second_back = back_pair[:, 1]
    slot_grad = jnp.stack(
        [first_weight[:, None] * upstream, second_weight[:, None] * upstream], axis=1
    )
    slot_grad = slot_grad.reshape(2 * tok_count, feature_count).astype(jnp.bfloat16)
    grad_send = jnp.dot(table_b, slot_grad, preferred_element_type=jnp.float32).astype(jnp.bfloat16)
    grad_rows = to_units(grad_send.reshape(expert_count, capacity, feature_count))
    unit_grad = lax.dot_general(
        grad_rows, down_weight[0], (((1,), (1,)), ((), ())), preferred_element_type=jnp.float32
    )
    sigma = jax.nn.sigmoid(gate_pre)
    gate_back = (unit_grad * up_pre * sigma * (1.0 + gate_pre * (1.0 - sigma))).astype(jnp.bfloat16)
    up_back = (unit_grad * jax.nn.silu(gate_pre)).astype(jnp.bfloat16)
    down_part = lax.dot_general(
        hidden, grad_rows, (((0,), (0,)), ((), ())), preferred_element_type=jnp.float32
    )
    gate_part = lax.dot_general(
        unit_rows, gate_back, (((0,), (0,)), ((), ())), preferred_element_type=jnp.float32
    )
    up_part = lax.dot_general(
        unit_rows, up_back, (((0,), (0,)), ((), ())), preferred_element_type=jnp.float32
    )
    gate_done = gate_part.astype(jnp.bfloat16)
    up_done = up_part.astype(jnp.bfloat16)
    down_done = down_part.astype(jnp.bfloat16)
    gate_side = lax.dot_general(
        gate_back, gate_weight[0], (((1,), (1,)), ((), ())), preferred_element_type=jnp.float32
    )
    up_side = lax.dot_general(
        up_back, up_weight[0], (((1,), (1,)), ((), ())), preferred_element_type=jnp.float32
    )
    returned = from_units(gate_side + up_side, expert_count)
    slot_back = lax.dot_general(
        table_b, returned, (((0,), (0,)), ((), ())), preferred_element_type=jnp.float32
    )
    slot_back = slot_back.reshape(tok_count, 2, feature_count)
    moe_grad = slot_back[:, 0] + slot_back[:, 1]
    gap_grad = first_weight * second_weight * (first_back - second_back)
    logit_grad = gap_grad[:, None] * (first_hot - second_hot)
    moe_in_grad = moe_grad + jnp.dot(logit_grad, router_weight.T, precision=HIGHEST)
    router_part = jnp.dot(moe_f.T, logit_grad, precision=HIGHEST)
    resid_grad = upstream + norm_back(resid_f, scale_two, moe_in_grad)
    zero_state = jnp.zeros_like(state_end)
    local_pull = mixer_pull((resid_grad, zero_state))
    later_grad = carry_states(decay_total, local_pull[3], True)
    tail_pull = mixer_pull((jnp.zeros_like(resid_grad), later_grad))
    normed_grad = local_pull[0] + tail_pull[0]
    rate_part = local_pull[1] + tail_pull[1]
    skip_part = local_pull[2] + tail_pull[2]
    token_grad = (resid_grad + norm_back(inputs, scale_one, normed_grad)).astype(jnp.bfloat16)
    router_total, rate_total, skip_total = in_one((router_part, rate_part, skip_part), "expert")
    return (
        block_out,
        token_grad,
        gate_done[None],
        up_done[None],
        down_done[None],
        router_total,
        rate_total,
        skip_total,
    )


def solution(mesh):
    return jax.shard_map(
        body,
        mesh=mesh,
        in_specs=(
            P("expert", "dp"),
            P("expert", None),
            P("expert", "dp"),
            P("expert", None),
            P("expert", None),
            P("dp"),
            P("dp"),
            P("dp", None),
            P("expert", None, "dp"),
            P("expert", None, "dp"),
            P("expert", "dp", None),
            P("expert", "dp"),
        ),
        out_specs=(
            P("expert", "dp"),
            P("expert", "dp"),
            P("expert", None, "dp"),
            P("expert", None, "dp"),
            P("expert", "dp", None),
            P("dp", None),
            P("dp"),
            P("dp"),
        ),
        check_vma=False,
    )
```

profile of v0, /device:TPU:1, one launch (start us, length us, event | category | flops | bytes accessed | tf_op | source)
XLA Modules:
  0.0 300.4 jit_solution(3704245302433064097)
XLA Ops:
  2.3 6.9 %all-to-all-start = ((f32[16,128,1]{1,2,0:T(1,128)}), f32[16,128,1]{1,2,0:T(1,128)S(1)}, u32[]{:S(2)}, u32[]{:S(2)}) async-start(f32[16,128,1]{1,2,0:T(1,128)} %broadcast_in_dim.186), calls=%async_computation | async-start | bytes 16384 | tf_op jit(solution)/shard_map/all_to_all | solution.py:15
  17.0 10.5 %all-to-all-start.1 = ((f32[16,3,1024]{2,1,0:T(4,128)}), f32[16,3,1024]{2,1,0:T(4,128)S(1)}, u32[]{:S(2)}, u32[]{:S(2)}) async-start(f32[16,3,1024]{2,1,0:T(4,128)} %broadcast_in_dim.190), calls=%async_computation.1 | async-start | bytes 524288 | tf_op jit(solution)/shard_map/all_to_all | solution.py:15
  28.1 9.7 %all-to-all-done.1 = f32[16,3,1024]{2,1,0:T(4,128)S(1)} async-done(((f32[16,3,1024]{2,1,0:T(4,128)}), f32[16,3,1024]{2,1,0:T(4,128)S(1)}, u32[]{:S(2)}, u32[]{:S(2)}) %all-to-all-start.1) | async-done | bytes 196640 | tf_op jit(solution)/shard_map/all_to_all | solution.py:15
  39.6 5.7 %all-to-all-start.2 = ((f32[16,128,1]{1,2,0:T(1,128)}), f32[16,128,1]{1,2,0:T(1,128)S(1)}, u32[]{:S(2)}, u32[]{:S(2)}) async-start(f32[16,128,1]{1,2,0:T(1,128)} %broadcast_in_dim.194), calls=%async_computation.2 | async-start | bytes 16384 | tf_op jit(solution)/shard_map/all_to_all | solution.py:15
  45.3 5.4 %all-to-all-done.2 = f32[16,128,1]{1,2,0:T(1,128)S(1)} async-done(((f32[16,128,1]{1,2,0:T(1,128)}), f32[16,128,1]{1,2,0:T(1,128)S(1)}, u32[]{:S(2)}, u32[]{:S(2)}) %all-to-all-start.2) | async-done | bytes 8224 | tf_op jit(solution)/shard_map/all_to_all | solution.py:15
  51.8 13.6 %all_to_all.86 = bf16[16,20,128]{2,1,0:T(8,128)(2,1)S(1)} all-to-all(bf16[16,20,128]{2,1,0:T(8,128)(2,1)S(1)} %reshape.365), channel_id=1, replica_groups=mesh['dp'=16,'expert'=16] {'expert'}, dimensions={0} | all-to-all | bytes 163840 | tf_op jit(solution)/shard_map/all_to_all | solution.py:185
  65.7 23.1 %all_to_all.87 = bf16[16,320,128]{2,1,0:T(8,128)(2,1)S(1)} all-to-all(bf16[16,320,128]{2,1,0:T(8,128)(2,1)S(1)} %broadcast_in_dim.200), channel_id=1, replica_groups=mesh['dp'=16,'expert'=16] {'dp'}, dimensions={0} | all-to-all | bytes 2621440 | tf_op jit(solution)/shard_map/all_to_all | solution.py:15
  94.8 4.6 %all-to-all-start.6 = ((bf16[16,320,128]{2,1,0:T(8,128)(2,1)}), bf16[16,320,128]{2,1,0:T(8,128)(2,1)S(1)}, u32[]{:S(2)}, u32[]{:S(2)}) async-start(bf16[16,320,128]{2,1,0:T(8,128)(2,1)} %bitcast.259), calls=%async_computation.6 | async-start | bytes 2621440 | tf_op jit(solution)/shard_map/all_to_all | solution.py:96
  101.8 16.2 %all-to-all-done.6 = bf16[16,320,128]{2,1,0:T(8,128)(2,1)S(1)} async-done(((bf16[16,320,128]{2,1,0:T(8,128)(2,1)}), bf16[16,320,128]{2,1,0:T(8,128)(2,1)S(1)}, u32[]{:S(2)}, u32[]{:S(2)}) %all-to-all-start.6) | async-done | bytes 1310752 | tf_op jit(solution)/shard_map/all_to_all | solution.py:96
  118.7 4.3 %all-to-all-start.3 = ((f32[16,128,16]{1,2,0:T(8,128)}), f32[16,128,16]{1,2,0:T(8,128)S(1)}, u32[]{:S(2)}, u32[]{:S(2)}) async-start(f32[16,128,16]{1,2,0:T(8,128)} %broadcast_in_dim.195), calls=%async_computation.3 | async-start | bytes 262144 | tf_op jit(solution)/shard_map/all_to_all | solution.py:15
  129.1 3.5 %all-to-all-start.7 = ((bf16[16,20,128]{2,1,0:T(8,128)(2,1)}), bf16[16,20,128]{2,1,0:T(8,128)(2,1)S(1)}, u32[]{:S(2)}, u32[]{:S(2)}) async-start(bf16[16,20,128]{2,1,0:T(8,128)(2,1)} %reshape.368), calls=%async_computation.7 | async-start | bytes 196608 | tf_op jit(solution)/shard_map/all_to_all | solution.py:193
  132.7 8.8 %all-to-all-done.7 = bf16[16,20,128]{2,1,0:T(8,128)(2,1)S(1)} async-done(((bf16[16,20,128]{2,1,0:T(8,128)(2,1)}), bf16[16,20,128]{2,1,0:T(8,128)(2,1)S(1)}, u32[]{:S(2)}, u32[]{:S(2)}) %all-to-all-start.7) | async-done | bytes 81952 | tf_op jit(solution)/shard_map/all_to_all | solution.py:193
  143.9 6.3 %all-to-all-start.12 = ((f32[16,128,2]{1,2,0:T(2,128)}), f32[16,128,2]{1,2,0:T(2,128)S(1)}, u32[]{:S(2)}, u32[]{:S(2)}) async-start(f32[16,128,2]{1,2,0:T(2,128)} %broadcast_in_dim.203), calls=%async_computation.12 | async-start | bytes 32768 | tf_op jit(solution)/shard_map/all_to_all | solution.py:15
  150.3 5.8 %all-to-all-done.12 = f32[16,128,2]{1,2,0:T(2,128)S(1)} async-done(((f32[16,128,2]{1,2,0:T(2,128)}), f32[16,128,2]{1,2,0:T(2,128)S(1)}, u32[]{:S(2)}, u32[]{:S(2)}) %all-to-all-start.12) | async-done | bytes 16416 | tf_op jit(solution)/shard_map/all_to_all | solution.py:15
  157.4 12.0 %all_to_all.88 = bf16[16,20,128]{2,1,0:T(8,128)(2,1)S(1)} all-to-all(bf16[16,20,128]{2,1,0:T(8,128)(2,1)S(1)} %reshape.370), channel_id=1, replica_groups=mesh['dp'=16,'expert'=16] {'expert'}, dimensions={0} | all-to-all | bytes 163840 | tf_op jit(solution)/shard_map/all_to_all | solution.py:185
  170.7 5.3 %all-to-all-start.9 = ((bf16[16,320,128]{2,1,0:T(8,128)(2,1)}), bf16[16,320,128]{2,1,0:T(8,128)(2,1)S(1)}, u32[]{:S(2)}, u32[]{:S(2)}) async-start(bf16[16,320,128]{2,1,0:T(8,128)(2,1)} %broadcast_in_dim.202), calls=%async_computation.9 | async-start | bytes 2621440 | tf_op jit(solution)/shard_map/all_to_all | solution.py:15
  176.5 18.1 %all-to-all-done.9 = bf16[16,320,128]{2,1,0:T(8,128)(2,1)S(1)} async-done(((bf16[16,320,128]{2,1,0:T(8,128)(2,1)}), bf16[16,320,128]{2,1,0:T(8,128)(2,1)S(1)}, u32[]{:S(2)}, u32[]{:S(2)}) %all-to-all-start.9) | async-done | bytes 1310752 | tf_op jit(solution)/shard_map/all_to_all | solution.py:15
  194.6 2.8 multiply_convert_fusion
  201.5 4.6 %all-to-all-start.10 = ((bf16[16,320,128]{2,1,0:T(8,128)(2,1)}), bf16[16,320,128]{2,1,0:T(8,128)(2,1)S(1)}, u32[]{:S(2)}, u32[]{:S(2)}) async-start(bf16[16,320,128]{2,1,0:T(8,128)(2,1)} %bitcast.258), calls=%async_computation.10 | async-start | bytes 2621440 | tf_op jit(solution)/shard_map/all_to_all | solution.py:96
  211.7 3.8 %fusion.1 = bf16[1,2048,448]{1,2,0:T(8,128)(2,1)} fusion(bf16[320,448]{1,0:T(8,128)(2,1)} %copy-done.10, bf16[16,320,128]{2,1,0:T(8,128)(2,1)} %copy-done.3), kind=kOutput, calls=%fused_computation.6 | convolution fusion | flops 588120064 | bytes 3432448 | tf_op jit(solution)/shard_map/dot_general | solution.py:271
  215.4 9.3 %all-to-all-done.10 = bf16[16,320,128]{2,1,0:T(8,128)(2,1)S(1)} async-done(((bf16[16,320,128]{2,1,0:T(8,128)(2,1)}), bf16[16,320,128]{2,1,0:T(8,128)(2,1)S(1)}, u32[]{:S(2)}, u32[]{:S(2)}) %all-to-all-start.10) | async-done | bytes 1310752 | tf_op jit(solution)/shard_map/all_to_all | solution.py:96
  225.6 3.5 %all-to-all-start.11 = ((bf16[16,20,128]{2,1,0:T(8,128)(2,1)}), bf16[16,20,128]{2,1,0:T(8,128)(2,1)S(1)}, u32[]{:S(2)}, u32[]{:S(2)}) async-start(bf16[16,20,128]{2,1,0:T(8,128)(2,1)} %reshape.373), calls=%async_computation.11 | async-start | bytes 196608 | tf_op jit(solution)/shard_map/all_to_all | solution.py:193
  229.2 3.9 %fusion.2 = bf16[1,2048,448]{1,2,0:T(8,128)(2,1)} fusion(bf16[320,448]{1,0:T(8,128)(2,1)} %copy-done.73, bf16[16,320,128]{2,1,0:T(8,128)(2,1)} %copy-done.3), kind=kOutput, calls=%fused_computation.7 | convolution fusion | flops 588120064 | bytes 3432448 | tf_op jit(solution)/shard_map/dot_general | solution.py:274
  233.0 5.0 %all-to-all-done.11 = bf16[16,20,128]{2,1,0:T(8,128)(2,1)S(1)} async-done(((bf16[16,20,128]{2,1,0:T(8,128)(2,1)}), bf16[16,20,128]{2,1,0:T(8,128)(2,1)S(1)}, u32[]{:S(2)}, u32[]{:S(2)}) %all-to-all-start.11) | async-done | bytes 81952 | tf_op jit(solution)/shard_map/all_to_all | solution.py:193
  241.4 5.3 %all-to-all-start.13 = ((f32[16,128,1]{1,2,0:T(1,128)}), f32[16,128,1]{1,2,0:T(1,128)S(1)}, u32[]{:S(2)}, u32[]{:S(2)}) async-start(f32[16,128,1]{1,2,0:T(1,128)} %broadcast_in_dim.204), calls=%async_computation.13 | async-start | bytes 16384 | tf_op jit(solution)/shard_map/all_to_all | solution.py:15
  246.7 3.3 %fusion.3 = bf16[1,448,2048]{2,1,0:T(8,128)(2,1)} fusion(bf16[320,448]{1,0:T(8,128)(2,1)} %copy-done.72, bf16[16,320,128]{2,1,0:T(8,128)(2,1)S(1)} %copy-done.5), kind=kOutput, calls=%fused_computation.8 | convolution fusion | flops 588120064 | bytes 3432448 | tf_op jit(solution)/shard_map/dot_general | solution.py:268
  250.1 2.1 all-to-all-done.13
  256.4 3.7 %all-to-all-start.14 = ((f32[16,3,1024]{2,1,0:T(4,128)}), f32[16,3,1024]{2,1,0:T(4,128)S(1)}, u32[]{:S(2)}, u32[]{:S(2)}) async-start(f32[16,3,1024]{2,1,0:T(4,128)} %broadcast_in_dim.206), calls=%async_computation.14 | async-start | bytes 524288 | tf_op jit(solution)/shard_map/all_to_all | solution.py:15
  264.7 5.7 %all-to-all-done.14 = f32[16,3,1024]{2,1,0:T(4,128)S(1)} async-done(((f32[16,3,1024]{2,1,0:T(4,128)}), f32[16,3,1024]{2,1,0:T(4,128)S(1)}, u32[]{:S(2)}, u32[]{:S(2)}) %all-to-all-start.14) | async-done | bytes 196640 | tf_op jit(solution)/shard_map/all_to_all | solution.py:15
  273.5 5.5 %all-to-all-start.15 = ((f32[16,128,1]{1,2,0:T(1,128)}), f32[16,128,1]{1,2,0:T(1,128)S(1)}, u32[]{:S(2)}, u32[]{:S(2)}) async-start(f32[16,128,1]{1,2,0:T(1,128)} %broadcast_in_dim.208), calls=%async_computation.15 | async-start | bytes 16384 | tf_op jit(solution)/shard_map/all_to_all | solution.py:15
  285.1 4.8 %all-to-all-start.16 = ((f32[16,1,2052]{2,1,0:T(1,128)}), f32[16,1,2052]{2,1,0:T(1,128)S(1)}, u32[]{:S(2)}, u32[]{:S(2)}) async-start(f32[16,1,2052]{2,1,0:T(1,128)} %broadcast_in_dim.212), calls=%async_computation.16 | async-start | bytes 278528 | tf_op jit(solution)/shard_map/all_to_all | solution.py:15
  290.8 8.1 %all-to-all-done.16 = f32[16,1,2052]{2,1,0:T(1,128)S(1)} async-done(((f32[16,1,2052]{2,1,0:T(1,128)}), f32[16,1,2052]{2,1,0:T(1,128)S(1)}, u32[]{:S(2)}, u32[]{:S(2)}) %all-to-all-start.16) | async-done | bytes 131360 | tf_op jit(solution)/shard_map/all_to_all | solution.py:15
  (347 shorter events, 67.4 us)
Async XLA Ops:
  0.6 91.9 %copy-start = (bf16[1,448,2048]{2,1,0:T(8,128)(2,1)S(1)}, bf16[1,448,2048]{2,1,0:T(8,128)(2,1)}, u32[]{:S(2)}) copy-start(bf16[1,448,2048]{2,1,0:T(8,128)(2,1)} %param.22) | copy-start | bytes 5505028
  2.3 12.3 %all-to-all-start = ((f32[16,128,1]{1,2,0:T(1,128)}), f32[16,128,1]{1,2,0:T(1,128)S(1)}, u32[]{:S(2)}, u32[]{:S(2)}) async-start(f32[16,128,1]{1,2,0:T(1,128)} %broadcast_in_dim.186), calls=%async_computation | async-start | bytes 16384 | tf_op jit(solution)/shard_map/all_to_all | solution.py:15
  10.0 28.3 %copy-start.27 = (f32[128,2]{0,1:T(2,128)}, f32[128,2]{0,1:T(2,128)S(1)}, u32[]{:S(2)}) copy-start(f32[128,2]{0,1:T(2,128)S(1)} %get-tuple-element.94) | copy-start | bytes 3076
  10.3 28.0 %copy-start.24 = (f32[128,2]{0,1:T(2,128)}, f32[128,2]{0,1:T(2,128)S(1)}, u32[]{:S(2)}) copy-start(f32[128,2]{0,1:T(2,128)S(1)} %copy.276) | copy-start | bytes 3076
  11.7 39.9 %copy-start.66 = (f32[256]{0:T(256)}, f32[256]{0:T(256)S(1)}, u32[]{:S(2)}) copy-start(f32[256]{0:T(256)S(1)} %compare_select_fusion.1) | copy-start | bytes 3076
  12.7 25.8 %copy-start.12 = (f32[128,128]{1,0:T(8,128)}, f32[128,128]{1,0:T(8,128)S(1)}, u32[]{:S(2)}) copy-start(f32[128,128]{1,0:T(8,128)S(1)} %fusion.160) | copy-start | bytes 196612
  15.2 23.5 %copy-start.18 = (f32[128,16]{0,1:T(8,128)S(1)}, f32[128,16]{0,1:T(8,128)}, u32[]{:S(2)}) copy-start(f32[128,16]{0,1:T(8,128)} %param.16) | copy-start | bytes 24580
  15.2 23.5 %copy-start.55 = (f32[2]{0:T(128)S(1)}, f32[2]{0:T(128)}, u32[]{:S(2)}) copy-start(f32[2]{0:T(128)} %param.18) | copy-start | bytes 28
  17.0 20.8 %all-to-all-start.1 = ((f32[16,3,1024]{2,1,0:T(4,128)}), f32[16,3,1024]{2,1,0:T(4,128)S(1)}, u32[]{:S(2)}, u32[]{:S(2)}) async-start(f32[16,3,1024]{2,1,0:T(4,128)} %broadcast_in_dim.190), calls=%async_computation.1 | async-start | bytes 524288 | tf_op jit(solution)/shard_map/all_to_all | solution.py:15
  27.6 37.8 %copy-start.38 = (f32[128,2]{0,1:T(2,128)}, f32[128,2]{0,1:T(2,128)S(1)}, u32[]{:S(2)}) copy-start(f32[128,2]{0,1:T(2,128)S(1)} %copy.278) | copy-start | bytes 3076
  38.5 27.2 %copy-start.19 = (f32[2,2,1024]{2,1,0:T(2,128)}, f32[2,2,1024]{2,1,0:T(2,128)S(1)}, u32[]{:S(2)}) copy-start(f32[2,2,1024]{2,1,0:T(2,128)S(1)} %slice_add_fusion.5) | copy-start | bytes 49156
  38.6 27.2 %copy-start.59 = (f32[2]{0:T(128)}, f32[2]{0:T(128)S(1)}, u32[]{:S(2)}) copy-start(f32[2]{0:T(128)S(1)} %slice_bitcast_fusion.5) | copy-start | bytes 28
  39.0 49.8 %copy-start.8 = (bf16[128,128]{0,1:T(8,128)(2,1)}, bf16[128,128]{0,1:T(8,128)(2,1)S(1)}, u32[]{:S(2)}) copy-start(bf16[128,128]{0,1:T(8,128)(2,1)S(1)} %get-tuple-element.92) | copy-start | bytes 98308
  39.6 11.2 %all-to-all-start.2 = ((f32[16,128,1]{1,2,0:T(1,128)}), f32[16,128,1]{1,2,0:T(1,128)S(1)}, u32[]{:S(2)}, u32[]{:S(2)}) async-start(f32[16,128,1]{1,2,0:T(1,128)} %broadcast_in_dim.194), calls=%async_computation.2 | async-start | bytes 16384 | tf_op jit(solution)/shard_map/all_to_all | solution.py:15
  45.3 43.5 %copy-start.62 = (f32[320]{0:T(512)}, f32[320]{0:T(512)S(1)}, u32[]{:S(2)}) copy-start(f32[320]{0:T(512)S(1)} %iota_convert_fusion) | copy-start | bytes 3844
  51.4 37.5 %copy-start.58 = (f32[128]{0:T(128)}, f32[128]{0:T(128)S(1)}, u32[]{:S(2)}) copy-start(f32[128]{0:T(128)S(1)} %get-tuple-element.118) | copy-start | bytes 1540
  94.8 23.2 %all-to-all-start.6 = ((bf16[16,320,128]{2,1,0:T(8,128)(2,1)}), bf16[16,320,128]{2,1,0:T(8,128)(2,1)S(1)}, u32[]{:S(2)}, u32[]{:S(2)}) async-start(bf16[16,320,128]{2,1,0:T(8,128)(2,1)} %bitcast.259), calls=%async_computation.6 | async-start | bytes 2621440 | tf_op jit(solution)/shard_map/all_to_all | solution.py:96
  118.7 10.5 %all-to-all-start.3 = ((f32[16,128,16]{1,2,0:T(8,128)}), f32[16,128,16]{1,2,0:T(8,128)S(1)}, u32[]{:S(2)}, u32[]{:S(2)}) async-start(f32[16,128,16]{1,2,0:T(8,128)} %broadcast_in_dim.195), calls=%async_computation.3 | async-start | bytes 262144 | tf_op jit(solution)/shard_map/all_to_all | solution.py:15
  126.7 30.4 %copy-start.63 = (f32[320]{0:T(512)S(1)}, f32[320]{0:T(512)}, u32[]{:S(2)}) copy-start(f32[320]{0:T(512)} %copy-done.62) | copy-start | bytes 3844
  126.7 30.4 %copy-start.67 = (f32[256]{0:T(256)S(1)}, f32[256]{0:T(256)}, u32[]{:S(2)}) copy-start(f32[256]{0:T(256)} %copy-done.66) | copy-start | bytes 3076
  129.1 12.4 %all-to-all-start.7 = ((bf16[16,20,128]{2,1,0:T(8,128)(2,1)}), bf16[16,20,128]{2,1,0:T(8,128)(2,1)S(1)}, u32[]{:S(2)}, u32[]{:S(2)}) async-start(bf16[16,20,128]{2,1,0:T(8,128)(2,1)} %reshape.368), calls=%async_computation.7 | async-start | bytes 196608 | tf_op jit(solution)/shard_map/all_to_all | solution.py:193
  132.6 24.3 %copy-start.41 = (s32[128]{0:T(128)}, s32[128]{0:T(128)S(1)}, u32[]{:S(2)}) copy-start(s32[128]{0:T(128)S(1)} %get-tuple-element.111) | copy-start | bytes 1540
  132.7 24.3 %copy-start.44 = (s32[128]{0:T(128)}, s32[128]{0:T(128)S(1)}, u32[]{:S(2)}) copy-start(s32[128]{0:T(128)S(1)} %get-tuple-element.112) | copy-start | bytes 1540
  143.9 12.1 %all-to-all-start.12 = ((f32[16,128,2]{1,2,0:T(2,128)}), f32[16,128,2]{1,2,0:T(2,128)S(1)}, u32[]{:S(2)}, u32[]{:S(2)}) async-start(f32[16,128,2]{1,2,0:T(2,128)} %broadcast_in_dim.203), calls=%async_computation.12 | async-start | bytes 32768 | tf_op jit(solution)/shard_map/all_to_all | solution.py:15
  156.1 54.7 %copy-start.49 = (f32[128]{0:T(128)}, f32[128]{0:T(128)S(1)}, u32[]{:S(2)}) copy-start(f32[128]{0:T(128)S(1)} %get-tuple-element.88) | copy-start | bytes 1540
  170.7 23.9 %all-to-all-start.9 = ((bf16[16,320,128]{2,1,0:T(8,128)(2,1)}), bf16[16,320,128]{2,1,0:T(8,128)(2,1)S(1)}, u32[]{:S(2)}, u32[]{:S(2)}) async-start(bf16[16,320,128]{2,1,0:T(8,128)(2,1)} %broadcast_in_dim.202), calls=%async_computation.9 | async-start | bytes 2621440 | tf_op jit(solution)/shard_map/all_to_all | solution.py:15
  201.5 23.2 %all-to-all-start.10 = ((bf16[16,320,128]{2,1,0:T(8,128)(2,1)}), bf16[16,320,128]{2,1,0:T(8,128)(2,1)S(1)}, u32[]{:S(2)}, u32[]{:S(2)}) async-start(bf16[16,320,128]{2,1,0:T(8,128)(2,1)} %bitcast.258), calls=%async_computation.10 | async-start | bytes 2621440 | tf_op jit(solution)/shard_map/all_to_all | solution.py:96
  225.6 12.5 %all-to-all-start.11 = ((bf16[16,20,128]{2,1,0:T(8,128)(2,1)}), bf16[16,20,128]{2,1,0:T(8,128)(2,1)S(1)}, u32[]{:S(2)}, u32[]{:S(2)}) async-start(bf16[16,20,128]{2,1,0:T(8,128)(2,1)} %reshape.373), calls=%async_computation.11 | async-start | bytes 196608 | tf_op jit(solution)/shard_map/all_to_all | solution.py:193
  241.4 10.8 %all-to-all-start.13 = ((f32[16,128,1]{1,2,0:T(1,128)}), f32[16,128,1]{1,2,0:T(1,128)S(1)}, u32[]{:S(2)}, u32[]{:S(2)}) async-start(f32[16,128,1]{1,2,0:T(1,128)} %broadcast_in_dim.204), calls=%async_computation.13 | async-start | bytes 16384 | tf_op jit(solution)/shard_map/all_to_all | solution.py:15
  256.4 14.1 %all-to-all-start.14 = ((f32[16,3,1024]{2,1,0:T(4,128)}), f32[16,3,1024]{2,1,0:T(4,128)S(1)}, u32[]{:S(2)}, u32[]{:S(2)}) async-start(f32[16,3,1024]{2,1,0:T(4,128)} %broadcast_in_dim.206), calls=%async_computation.14 | async-start | bytes 524288 | tf_op jit(solution)/shard_map/all_to_all | solution.py:15
  273.5 10.9 %all-to-all-start.15 = ((f32[16,128,1]{1,2,0:T(1,128)}), f32[16,128,1]{1,2,0:T(1,128)S(1)}, u32[]{:S(2)}, u32[]{:S(2)}) async-start(f32[16,128,1]{1,2,0:T(1,128)} %broadcast_in_dim.208), calls=%async_computation.15 | async-start | bytes 16384 | tf_op jit(solution)/shard_map/all_to_all | solution.py:15
  285.1 13.8 %all-to-all-start.16 = ((f32[16,1,2052]{2,1,0:T(1,128)}), f32[16,1,2052]{2,1,0:T(1,128)S(1)}, u32[]{:S(2)}, u32[]{:S(2)}) async-start(f32[16,1,2052]{2,1,0:T(1,128)} %broadcast_in_dim.212), calls=%async_computation.16 | async-start | bytes 278528 | tf_op jit(solution)/shard_map/all_to_all | solution.py:15
  (58 other events, 482.3 us)
where the time goes:
time: 303 us; the launch traced here: 300 us
  waiting for transfers between devices  97.8 us (32%)
  starting transfers between devices  74.4 us (25%)
  blocking collectives  48.6 us (16%)
  matrix products  31.7 us (10%)
  local copies, waits for them, and re-layouts  28.7 us (9%)
  other arithmetic  17.1 us (6%)
    all_to_all x10, waiting for transfers between devices, sent_to_all(): lax.all_to_all(jnp.broadcast_to(x[None], (peers, *x.shape)), axis, 0, 0,...  58.6 us
    all_to_all x10, starting transfers between devices, sent_to_all(): lax.all_to_all(jnp.broadcast_to(x[None], (peers, *x.shape)), axis, 0, 0,...  58.2 us
    all_to_all x2, blocking collectives, to_units(): lax.all_to_all(send_rows, 'expert', split_axis=0, concat_axis=0, tiled=True)  25.6 us
    all_to_all x2, waiting for transfers between devices, sent_and_summed(): tiles = lax.all_to_all(split_up(x, dim, peers), axis, 0, 0, tiled=True)  25.5 us
    all_to_all x1, blocking collectives, sent_to_all(): lax.all_to_all(jnp.broadcast_to(x[None], (peers, *x.shape)), axis, 0, 0,...  23.1 us
    all_to_all x2, waiting for transfers between devices, from_units(): lax.all_to_all(shaped, 'expert', split_axis=0, concat_axis=0, tiled=True)  13.8 us
    all_to_all x2, starting transfers between devices, sent_and_summed(): tiles = lax.all_to_all(split_up(x, dim, peers), axis, 0, 0, tiled=True)  9.15 us
    broadcast_in_dim x13, local copies, waits for them, and re-layouts, sent_to_all(): jnp.broadcast_to(x[None], (peers, *x.shape))  7.53 us
  transfers between devices with their start and end apart: 14, of which 14 were waited for; matrix products, arithmetic and copies ran while one was open for 13% of the time, Pallas kernels for 0%

commit v1 on v0

v1 whole, which is shorter than its diff:
```python
import functools

import jax
import jax.numpy as jnp
from jax import lax
from jax.experimental import pallas as pl
from jax.experimental.pallas import tpu as pltpu
from jax.sharding import PartitionSpec as P

EPSILON = 1e-06
CAPACITY = 20
SLOT_PAD = 32
HIGH = lax.Precision.HIGHEST
F32 = jnp.float32
BF16 = jnp.bfloat16
MESH = pl.DeviceIdType.MESH
NN = (((1,), (0,)), ((), ()))
NT = (((1,), (1,)), ((), ()))


def mm(a, b, dims=NN, precision=None):
    return lax.dot_general(a, b, dims, precision=precision, preferred_element_type=F32)


def iota(shape, dim):
    return lax.broadcasted_iota(jnp.int32, shape, dim)


def remote(src, dst, send_sem, recv_sem, axis, peer):
    return pltpu.make_async_remote_copy(
        src_ref=src,
        dst_ref=dst,
        send_sem=send_sem,
        recv_sem=recv_sem,
        device_id={axis: peer},
        device_id_type=MESH,
    )


class Exchange:
    def __init__(self, axis, me, size, src, dst, sems, same=False):
        self.axis, self.me, self.size = axis, me, size
        self.src, self.dst, self.sems, self.same = src, dst, sems, same

    def copy(self, peer):
        src = self.dst.at[self.me] if self.same else self.src.at[peer]
        return remote(
            src, self.dst.at[self.me], self.sems.at[0, peer], self.sems.at[1, self.me], self.axis, peer
        )

    def arrival(self, peer):
        spot = self.dst.at[peer]
        return remote(spot, spot, self.sems.at[0, peer], self.sems.at[1, peer], self.axis, peer)

    def each(self, act, low=None, high=None):
        if low is None:
            def step(k, carry):
                act(lax.rem(self.me + k, self.size))
                return carry

            lax.fori_loop(1, self.size, step, 0)
        else:
            def step(p, carry):
                act(p)
                return carry

            lax.fori_loop(low, high, step, 0)

    def start(self, low=None, high=None):
        self.each(lambda p: self.copy(p).start(), low, high)

    def wait(self, low=None, high=None):
        self.each(lambda p: self.arrival(p).wait_recv(), low, high)

    def drain(self, low=None, high=None):
        self.each(lambda p: self.copy(p).wait_send(), low, high)


def block_kernel(
    dims,
    x_ref,
    routes_ref,
    dt_ref,
    b_ref,
    c_ref,
    rate_ref,
    skip_ref,
    rw_ref,
    og_ref,
    wg_hbm,
    wu_hbm,
    wd_hbm,
    block_ref,
    token_ref,
    router_ref,
    small_ref,
    u_hbm,
    g_hbm,
    gt_hbm,
    ut_hbm,
    ht_hbm,
    wg,
    wu,
    wd,
    rows_u,
    rows_g,
    gacc,
    uacc,
    vacc,
    hid,
    gb,
    ub,
    gs,
    us,
    hs,
    gst,
    ust,
    hst,
    cols,
    zrow,
    keep,
    pair_out,
    pair_in,
    rs_out,
    rs_in,
    ar1,
    ar2,
    ar3,
    ar4,
    dec,
    st,
    dl,
    sg,
    tot,
    rout,
    og_out,
    og_in,
    xs_out,
    xs_in,
    sq_out,
    sq_in,
    sb_out,
    sb_in,
    bk_out,
    bk_in,
    mt,
    spread,
    local_sem,
    ag_sem,
    pair_sem,
    rs_sem,
    sem_d,
    sem_e,
):
    nd, ne, t_n, f_n, d_all, cap = dims
    pad = SLOT_PAD
    heads = dt_ref.shape[0]
    hp = f_n // heads
    n_state = b_ref.shape[0]
    rows = ne * cap
    spots = ne * pad
    chips = nd // 2
    ny = min(4, chips)
    nx = chips // ny
    me_d = lax.axis_index("dp")
    me_e = lax.axis_index("expert")
    core = lax.rem(me_d, 2)
    chip = me_d // 2
    chip_x, chip_y = chip // ny, lax.rem(chip, ny)
    partner = me_d + 1 - 2 * core

    def chip_after(i):
        return lax.rem(chip_x + i // ny, nx) * ny + lax.rem(chip_y + lax.rem(i, ny), ny)

    def chip_before(i):
        return lax.rem(chip_x + nx - i // ny, nx) * ny + lax.rem(chip_y + ny - lax.rem(i, ny), ny)

    weight_copies = [
        pltpu.make_async_copy(src, dst, local_sem.at[k])
        for k, (src, dst) in enumerate(((wd_hbm, wd), (wg_hbm, wg), (wu_hbm, wu)))
    ]
    for copy in weight_copies:
        copy.start()

    barrier = pltpu.get_barrier_semaphore()

    def greet(axis, me, size):
        def step(k, carry):
            pl.semaphore_signal(
                barrier, inc=1, device_id={axis: lax.rem(me + k, size)}, device_id_type=MESH
            )
            return carry

        lax.fori_loop(1, size, step, 0)

    greet("dp", me_d, nd)
    greet("expert", me_e, ne)

    def on_dp(dst, k):
        return Exchange("dp", me_d, nd, None, dst, sem_d.at[k], same=True)

    def on_expert(dst, k, src=None):
        return Exchange("expert", me_e, ne, src, dst, sem_e.at[k], same=src is None)

    ex_ar1, ex_ar2, ex_ar3, ex_ar4 = (on_dp(r, k) for k, r in enumerate((ar1, ar2, ar3, ar4)))
    ex_dec, ex_st, ex_dl, ex_sg, ex_tot, ex_rout = (
        on_expert(r, k) for k, r in enumerate((dec, st, dl, sg, tot, rout))
    )
    ex_og = on_expert(og_in, 6, og_out)
    ex_xs = on_expert(xs_in, 7, xs_out)
    ex_sq = on_expert(sq_in, 8, sq_out)
    ex_sb = on_expert(sb_in, 9, sb_out)
    ex_bk = [on_expert(bk_in.at[k], 10 + k, bk_out.at[k]) for k in range(2)]

    x_t = x_ref[...].astype(F32).T
    ar1[me_d] = jnp.sum(x_t * x_t, axis=0, keepdims=True)
    row_id, col_id = iota((t_n, t_n), 0), iota((t_n, t_n), 1)
    causal = row_id <= col_id
    step_size = jnp.maximum(dt_ref[...], 0.0) + jnp.log1p(jnp.exp(-jnp.abs(dt_ref[...])))
    cum = mm(step_size, causal.astype(F32), NN, HIGH)
    head_lane = iota((1, f_n), 1) < hp
    head_row = iota((f_n, t_n), 0) < hp
    last = [jnp.sum(step_size[h : h + 1], axis=1, keepdims=True) for h in range(heads)]
    fade = [jnp.exp(-rate_ref[h] * last[h]) for h in range(heads)]
    dec[me_e] = jnp.concatenate(
        [
            jnp.where(head_lane, fade[0], fade[1]),
            jnp.where(head_lane, -last[0] * fade[0], -last[1] * fade[1]),
        ],
        axis=0,
    )

    expert_row = iota((ne, t_n), 0)
    hot_a = (expert_row == routes_ref[0:1, :]).astype(F32)
    hot_b = (expert_row == routes_ref[1:2, :]).astype(F32)
    before = mm((hot_a + hot_b).astype(BF16), (row_id < col_id).astype(BF16))
    spread_rows = (iota((spots, ne), 0) // pad == iota((spots, ne), 1)).astype(BF16)
    slot_of = iota((spots, t_n), 0) % pad
    fits = slot_of < cap
    here = (mm(spread_rows, before.astype(BF16)) == slot_of.astype(F32)) & fits
    pick_a = jnp.where(here, mm(spread_rows, hot_a.astype(BF16)), 0.0)
    pick_b = jnp.where(here, mm(spread_rows, hot_b.astype(BF16)), 0.0)
    pick = (pick_a + pick_b).astype(BF16)
    og = og_ref[...]
    og_out[...] = mm(pick, og).astype(BF16).reshape(ne, pad, f_n)
    og_in[me_e] = og_out[me_e]

    pl.semaphore_wait(barrier, nd + ne - 2)
    ex_ar1.start()
    ex_og.start()
    ex_dec.start()

    b_rows, c_rows = b_ref[...], c_ref[...]
    pairing = mm(b_rows.T, c_rows, NN, HIGH)
    fades, tails = [], []
    for h in range(heads):
        cum_h, dt_h = cum[h : h + 1], step_size[h : h + 1]
        gap = jnp.where(causal, cum_h - jnp.broadcast_to(cum_h, (t_n, t_n)).T, 0.0)
        spread[h] = gap
        mt[h] = (
            jnp.where(causal, jnp.exp(-rate_ref[h] * gap), 0.0)
            * pairing
            * jnp.broadcast_to(dt_h, (t_n, t_n)).T
        )
        fades.append(jnp.exp(-rate_ref[h] * cum_h))
        tails.append(jnp.exp(-rate_ref[h] * (last[h] - cum_h)) * dt_h)
    tail = jnp.where(head_row, tails[0], tails[1])
    reach = jnp.where(head_row, cum[0:1] - last[0], cum[1:2] - last[1])
    skip_f = jnp.where(head_row, skip_ref[0], skip_ref[1])
    hot_gap = hot_a - hot_b
    rw_gap = mm(rw_ref[...].T, hot_gap, NN, HIGH)
    spot_q = iota((rows, spots), 1)
    compact = (
        ((spot_q // pad) * cap + spot_q % pad == iota((rows, spots), 0)) & (spot_q % pad < cap)
    ).astype(BF16)
    of_block_r, of_block_b = iota((rows, ne), 0), iota((rows, ne), 1) * cap
    of_block = ((of_block_r >= of_block_b) & (of_block_r < of_block_b + cap)).astype(F32)
    lane_r = iota((rows, 128), 0)
    slot_r = lane_r - (lane_r * ((1 << 20) // cap + 1) >> 20) * cap
    lane_first = iota((rows, 128), 1) == slot_r
    lane_second = iota((rows, 128), 1) == slot_r + 64

    ex_ar1.wait()
    scale_one = lax.rsqrt(jnp.sum(ar1[...], axis=0) / d_all + EPSILON)
    normed = x_t * scale_one
    st[me_e] = mm(b_rows, normed * tail, NT, HIGH)
    ex_st.start(me_e + 1, ne)
    dl[me_e] = mm(b_rows, normed * tail * reach, NT, HIGH)
    ex_dl.start(me_e + 1, ne)
    mixed = jnp.concatenate(
        [mm(normed[h * hp : (h + 1) * hp], mt[h], NN, HIGH) for h in range(heads)], axis=0
    )
    mixed = mixed + skip_f * normed

    def ag_begin(buf, k):
        def step(i, carry):
            peer = chip_after(i) * 2 + core
            remote(
                buf.at[me_d], buf.at[me_d], ag_sem.at[k, 0, i], ag_sem.at[k, 1, i], "dp", peer
            ).start()
            return carry

        remote(
            buf.at[me_d], buf.at[me_d], ag_sem.at[k, 2, 0], ag_sem.at[k, 3, 0], "dp", partner
        ).start()
        lax.fori_loop(1, chips, step, 0)

    def ag_forward(buf, k, i):
        spot = buf.at[chip_before(i) * 2 + core]
        remote(
            spot, spot, ag_sem.at[k, 0, i], ag_sem.at[k, 1, i], "dp", chip_before(i) * 2 + core
        ).wait_recv()
        remote(spot, spot, ag_sem.at[k, 2, i], ag_sem.at[k, 3, i], "dp", partner).start()

    def ag_partner(buf, k, i):
        spot = buf.at[chip_before(i) * 2 + 1 - core]
        remote(spot, spot, ag_sem.at[k, 2, i], ag_sem.at[k, 3, i], "dp", partner).wait_recv()

    def ag_drain(buf, k):
        def step(i, carry):
            remote(
                buf.at[me_d], buf.at[me_d], ag_sem.at[k, 0, i], ag_sem.at[k, 1, i], "dp", chip_after(i) * 2 + core
            ).wait_send()
            spot = buf.at[chip_before(i) * 2 + core]
            remote(spot, spot, ag_sem.at[k, 2, i], ag_sem.at[k, 3, i], "dp", partner).wait_send()
            return carry

        remote(
            buf.at[me_d], buf.at[me_d], ag_sem.at[k, 2, 0], ag_sem.at[k, 3, 0], "dp", partner
        ).wait_send()
        lax.fori_loop(1, chips, step, 0)

    def ag_consume(buf, k, use):
        def step(i, carry):
            @pl.when(i < chips)
            def _():
                ag_forward(buf, k, i)

            ag_partner(buf, k, i - 1)
            j = chip_before(i - 1)
            both = jnp.concatenate([buf[2 * j], buf[2 * j + 1]], axis=1)
            use(both, pl.ds(pl.multiple_of(j * 2 * f_n, 2 * f_n), 2 * f_n))
            return carry

        lax.fori_loop(1, chips + 1, step, 0)

    ex_og.wait()
    rows_g[me_d] = mm(compact, og_in[...].reshape(spots, f_n)).astype(BF16)
    ag_begin(rows_g, 0)

    ex_dec.wait()

    def carry_state(j, state):
        ex_st.arrival(j).wait_recv()
        return dec[j][0:1] * state + st[j]

    state_in = lax.fori_loop(0, me_e, carry_state, jnp.zeros((n_state, f_n), F32))
    state_col = state_in.T
    from_state = jnp.concatenate(
        [mm(state_col[h * hp : (h + 1) * hp], c_rows * fades[h], NN, HIGH) for h in range(heads)],
        axis=0,
    )
    resid_t = (x_t + (mixed + from_state)).astype(BF16).astype(F32)
    resid = resid_t.T.astype(BF16)
    ar2[me_d] = jnp.concatenate(
        [
            jnp.sum(resid_t * resid_t, axis=0, keepdims=True),
            jnp.sum(resid_t * rw_gap, axis=0, keepdims=True),
        ],
        axis=0,
    )
    ex_ar2.start()
    xs_out[...] = mm(pick, resid).astype(BF16).reshape(ne, pad, f_n)
    xs_in[me_e] = xs_out[me_e]
    ex_xs.start()

    def carry_slope(j, both):
        state, slope = both
        ex_dl.arrival(j).wait_recv()
        here_dec = dec[j]
        return (
            here_dec[0:1] * state + st[j],
            here_dec[0:1] * slope + here_dec[1:2] * state + dl[j],
        )

    zero_state = jnp.zeros((n_state, f_n), F32)
    slope_in = lax.fori_loop(0, me_e, carry_slope, (zero_state, zero_state))[1]

    ex_ar2.wait()
    sums = jnp.sum(ar2[...], axis=0)
    scale_two = lax.rsqrt(sums[0:1] / d_all + EPSILON)
    gap_raw = sums[1:2]
    logit_gap = scale_two * gap_raw
    first_w = 1.0 / (1.0 + jnp.exp(-logit_gap))
    second_w = 1.0 / (1.0 + jnp.exp(logit_gap))
    scale_col = jnp.sum((pick_a + pick_b) * scale_two, axis=1, keepdims=True)
    weight_col = jnp.sum(pick_a * first_w + pick_b * second_w, axis=1, keepdims=True)
    lane_q = iota((spots, 128), 1)
    slot_q = iota((spots, 128), 0) % pad
    lined = jnp.where(lane_q == slot_q, scale_col, 0.0) + jnp.where(
        lane_q == slot_q + 64, weight_col, 0.0
    )
    lined = jnp.sum(lined.reshape(ne, pad, 128), axis=1)
    for e in range(ne):
        sq_out[e] = lined[e : e + 1]
    sq_in[me_e] = sq_out[me_e]
    ex_sq.start()

    weight_copies[0].wait()
    vacc[...] = jnp.zeros_like(vacc)

    def use_grad(both, span):
        vacc[...] += mm(both, wd[:, span], NT)

    ag_consume(rows_g, 0, use_grad)

    ex_xs.wait()
    rows_u[me_d] = mm(compact, xs_in[...].reshape(spots, f_n)).astype(BF16)
    ag_begin(rows_u, 1)
    weight_copies[1].wait()
    weight_copies[2].wait()
    gacc[...] = jnp.zeros_like(gacc)
    uacc[...] = jnp.zeros_like(uacc)
    ex_sq.wait()

    def by_row(ref):
        table = jnp.concatenate([ref[b] for b in range(ne)], axis=0)
        return mm(of_block, table, NN, HIGH)

    wide = by_row(sq_in)
    cols[0] = jnp.sum(jnp.where(lane_first, wide, 0.0), axis=1, keepdims=True)
    cols[1] = jnp.sum(jnp.where(lane_second, wide, 0.0), axis=1, keepdims=True)

    def use_rows(both, span):
        gacc[...] += mm(both, wg[:, span], NT)
        uacc[...] += mm(both, wu[:, span], NT)

    ag_consume(rows_u, 1, use_rows)
    out_copies = [
        pltpu.make_async_copy(rows_g, g_hbm, local_sem.at[3]),
        pltpu.make_async_copy(rows_u, u_hbm, local_sem.at[4]),
    ]
    for copy in out_copies:
        copy.start()

    part = rows // 5

    def units(k, carry):
        span = pl.ds(pl.multiple_of(k * part, part), part)
        scale, weight = cols[0, span], cols[1, span]
        gate_in, up_in, grad_in = gacc[span], uacc[span], vacc[span]
        gate, up, grad = gate_in * scale, up_in * scale, grad_in * weight
        sigma = 1.0 / (1.0 + jnp.exp(-gate))
        silu = gate * sigma
        hidden = silu * up
        gate_back = grad * up * sigma * (1.0 + gate * (1.0 - sigma))
        up_back = grad * silu
        hid[span] = hidden.astype(BF16)
        gb[span] = gate_back.astype(BF16)
        ub[span] = up_back.astype(BF16)
        gs[span] = gate_back * scale
        us[span] = up_back * scale
        hs[span] = hidden * weight
        pair_sum = jnp.sum(hidden * grad_in, axis=1, keepdims=True)
        inner_sum = jnp.sum(gate_back * gate_in + up_back * up_in, axis=1, keepdims=True)
        lane = iota((part, 128), 1)
        row_r = iota((part, 128), 0) + k * part
        slot = row_r - (row_r * ((1 << 20) // cap + 1) >> 20) * cap
        zrow[span] = jnp.where(lane == slot, pair_sum, 0.0) + jnp.where(
            lane == slot + 64, inner_sum, 0.0
        )
        return carry

    lax.fori_loop(0, 5, units, 0)
    block_t_b, block_t_r = iota((ne, rows), 0) * cap, iota((ne, rows), 1)
    of_block_t = ((block_t_r >= block_t_b) & (block_t_r < block_t_b + cap)).astype(F32)
    ar3[me_d] = mm(of_block_t, zrow[...], NN, HIGH)
    ex_ar3.start()

    def rs_pass(k, terms):
        def finish(i):
            j = chip_after(i)
            remote(
                pair_in.at[k, j], pair_in.at[k, j], pair_sem.at[k, 0, j], pair_sem.at[k, 1, j], "dp", partner
            ).wait_recv()
            total = keep[k, j] + pair_in[k, j].astype(F32)
            rs_out[k, i] = total.astype(BF16)

            @pl.when(i > 0)
            def _():
                rs_copy(k, i).start()

        def step(n, carry):
            @pl.when(n < chips)
            def _():
                i = lax.rem(n + 1, chips)
                j = chip_after(i)
                both = terms(pl.ds(pl.multiple_of(j * 2 * f_n, 2 * f_n), 2 * f_n))
                low, high = both[:, :f_n], both[:, f_n:]
                first = core == 0
                keep[k, j] = jnp.where(first, low, high)
                pair_out[k, j] = jnp.where(first, high, low).astype(BF16)
                pair_copy(k, j).start()

            @pl.when(n > 0)
            def _():
                finish(lax.rem(n, chips))

            return carry

        lax.fori_loop(0, chips + 1, step, 0)

    def pair_copy(k, j):
        return remote(
            pair_out.at[k, j], pair_in.at[k, j], pair_sem.at[k, 0, j], pair_sem.at[k, 1, j], "dp", partner
        )

    def rs_copy(k, i):
        return remote(
            rs_out.at[k, i], rs_in.at[k, i], rs_sem.at[k, 0, i], rs_sem.at[k, 1, i], "dp", chip_after(i) * 2 + core
        )

    rs_pass(0, lambda span: mm(hid[...], wd[:, span]))
    rs_pass(1, lambda span: mm(gb[...], wg[:, span]) + mm(ub[...], wu[:, span]))

    ex_ar3.wait()
    line = jnp.sum(ar3[...], axis=0)
    for b in range(ne):
        sb_out[b] = line[b : b + 1]
    sb_in[me_e] = sb_out[me_e]
    ex_sb.start()

    for k, (src, dst, out) in enumerate(((gs, gst, gt_hbm), (us, ust, ut_hbm), (hs, hst, ht_hbm))):
        dst[...] = src[...].T.astype(BF16)
        copy = pltpu.make_async_copy(dst, out, local_sem.at[5 + k])
        copy.start()
        out_copies.append(copy)

    def rs_finish(k):
        def step(i, total):
            remote(
                rs_in.at[k, i], rs_in.at[k, i], rs_sem.at[k, 0, i], rs_sem.at[k, 1, i], "dp", chip_before(i) * 2 + core
            ).wait_recv()
            return total + rs_in[k, i].astype(F32)

        total = lax.fori_loop(1, chips, step, rs_out[k, 0].astype(F32))
        wide_rows = lax.dot_general(
            compact, total.astype(BF16), (((0,), (0,)), ((), ())), preferred_element_type=F32
        )
        bk_out[k] = wide_rows.astype(BF16).reshape(ne, pad, f_n)
        bk_in[k, me_e] = bk_out[k, me_e]
        ex_bk[k].start()

    rs_finish(0)

    ex_sb.wait()
    table = jnp.concatenate([sb_in[e] for e in range(ne)], axis=0)
    by_spot = mm(spread_rows.astype(F32), table, NN, HIGH)
    pair_spot = jnp.sum(jnp.where(lane_q == slot_q, by_spot, 0.0), axis=1, keepdims=True)
    inner_spot = jnp.sum(jnp.where(lane_q == slot_q + 64, by_spot, 0.0), axis=1, keepdims=True)
    back_gap = jnp.sum((pick_a - pick_b) * pair_spot, axis=0, keepdims=True)
    inner_two = jnp.sum((pick_a + pick_b) * inner_spot, axis=0, keepdims=True)
    gap_grad = first_w * second_w * back_gap
    inner_two = inner_two + gap_grad * gap_raw
    rout[me_e] = mm(hot_gap * (gap_grad * scale_two), resid_t, NT, HIGH)
    ex_rout.start()

    pick_at, pick_bt = pick_a.T.astype(BF16), pick_b.T.astype(BF16)
    resid_base = og.astype(F32).T + scale_two * (gap_grad * rw_gap) - resid_t * (
        scale_two * scale_two * scale_two * inner_two / d_all
    )
    first_m = jnp.broadcast_to(first_w, (f_n, t_n)).T
    second_m = jnp.broadcast_to(second_w, (f_n, t_n)).T

    rs_finish(1)
    ex_bk[0].wait()
    came = bk_in[0].reshape(spots, f_n)
    block_ref[...] = (
        resid.astype(F32) + (first_m * mm(pick_at, came) + second_m * mm(pick_bt, came))
    ).astype(BF16)

    ex_bk[1].wait()
    moe_grad = mm(pick_at + pick_bt, bk_in[1].reshape(spots, f_n)).T
    grad = resid_base + scale_two * moe_grad
    state_grads = [mm(c_rows * fades[h], grad, NT, HIGH) for h in range(heads)]
    state_grad = jnp.where(head_lane, state_grads[0], state_grads[1])
    sg[me_e] = state_grad
    ex_sg.start(0, me_e)

    normed_rows = normed.T
    cum_f = jnp.where(head_row, cum[0:1], cum[1:2])
    rate_row = jnp.sum(state_grad * slope_in, axis=0, keepdims=True)
    state_part = grad * from_state * cum_f
    skip_part = grad * normed
    lane_s = iota((1, 128), 1)
    small = jnp.zeros((1, 128), F32)
    for h in range(heads):
        mine = head_row if h == 0 else jnp.logical_not(head_row)
        mine_lane = head_lane if h == 0 else jnp.logical_not(head_lane)
        pair_grad = mm(normed_rows, jnp.where(mine, grad, 0.0), NN, HIGH)
        table_part = pair_grad * mt[h] * spread[h]
        rows_h = slice(h * hp, (h + 1) * hp)
        rate_h = (
            jnp.sum(jnp.where(mine_lane, rate_row, 0.0), axis=1, keepdims=True)
            - jnp.sum(jnp.sum(table_part, axis=0, keepdims=True), axis=1, keepdims=True)
            - jnp.sum(jnp.sum(state_part[rows_h], axis=0, keepdims=True), axis=1, keepdims=True)
        )
        skip_h = jnp.sum(jnp.sum(skip_part[rows_h], axis=0, keepdims=True), axis=1, keepdims=True)
        small = small + jnp.where(lane_s == h, rate_h, 0.0)
        small = small + jnp.where(lane_s == heads + h, skip_h, 0.0)
    tot[me_e] = small
    ex_tot.start()
    normed_grad = jnp.concatenate(
        [mm(grad[h * hp : (h + 1) * hp], mt[h], NT, HIGH) for h in range(heads)], axis=0
    )
    normed_grad = normed_grad + skip_f * grad

    def carry_grad(n, later):
        j = ne - 1 - n
        ex_sg.arrival(j).wait_recv()
        return dec[j][0:1] * later + sg[j]

    later = lax.fori_loop(0, ne - 1 - me_e, carry_grad, zero_state)
    normed_grad = normed_grad + tail * mm(later.T, b_rows, NN, HIGH)
    ar4[me_d] = jnp.sum(normed_grad * x_t, axis=0, keepdims=True)
    ex_ar4.start()
    ex_rout.wait()
    router_ref[...] = jnp.sum(rout[...], axis=0)
    ex_ar4.wait()
    inner_one = jnp.sum(ar4[...], axis=0)
    token_grad = (
        grad + scale_one * normed_grad - x_t * (scale_one * scale_one * scale_one * inner_one / d_all)
    )
    token_ref[...] = token_grad.T.astype(BF16)
    ex_tot.wait()
    small_ref[...] = jnp.sum(tot[...], axis=0)

    for ex in (ex_ar1, ex_ar2, ex_ar3, ex_ar4, ex_dec, ex_tot, ex_rout, ex_og, ex_xs, ex_sq, ex_sb, *ex_bk):
        ex.drain()
    ex_st.drain(me_e + 1, ne)
    ex_dl.drain(me_e + 1, ne)
    ex_sg.drain(0, me_e)
    ag_drain(rows_g, 0)
    ag_drain(rows_u, 1)
    for k in range(2):
        def step(i, carry, k=k):
            pair_copy(k, i).wait_send()

            @pl.when(i > 0)
            def _():
                rs_copy(k, i).wait_send()

            return carry

        lax.fori_loop(0, chips, step, 0)
    for copy in out_copies:
        copy.wait()


def grads_kernel(u_ref, g_ref, gt_ref, ut_ref, ht_ref, gate_ref, up_ref, down_ref):
    both_u = jnp.concatenate([u_ref[0], u_ref[1]], axis=1)
    both_g = jnp.concatenate([g_ref[0], g_ref[1]], axis=1)
    gate_ref[...] = mm(gt_ref[...], both_u).astype(BF16)
    up_ref[...] = mm(ut_ref[...], both_u).astype(BF16)
    down_ref[...] = mm(ht_ref[...], both_g).astype(BF16)


def body(
    tokens,
    routes,
    dt_raw,
    b_proj,
    c_proj,
    decay_rate,
    skip_gain,
    router_weight,
    gate_weight,
    up_weight,
    down_weight,
    out_grad,
):
    nd, ne = lax.axis_size("dp"), lax.axis_size("expert")
    t_n, f_n = tokens.shape
    heads, n_state = dt_raw.shape[1], b_proj.shape[1]
    d_all = nd * f_n
    units = down_weight.shape[1]
    cap, pad = CAPACITY, SLOT_PAD
    rows, chips = ne * cap, nd // 2
    vmem, hbm, smem = (
        pl.BlockSpec(memory_space=space) for space in (pltpu.VMEM, pl.ANY, pltpu.SMEM)
    )
    def v(*s):
        return pltpu.VMEM(s, F32)

    def h(*s):
        return pltpu.VMEM(s, BF16)

    def shape(s, t):
        return jax.ShapeDtypeStruct(s, t)
    scratch = [
        h(units, d_all),
        h(units, d_all),
        h(units, d_all),
        h(nd, rows, f_n),
        h(nd, rows, f_n),
        v(rows, units),
        v(rows, units),
        v(rows, units),
        h(rows, units),
        h(rows, units),
        h(rows, units),
        v(rows, units),
        v(rows, units),
        v(rows, units),
        h(units, rows),
        h(units, rows),
        h(units, rows),
        v(2, rows, 1),
        v(rows, 128),
        v(2, chips, rows, f_n),
        h(2, chips, rows, f_n),
        h(2, chips, rows, f_n),
        h(2, chips, rows, f_n),
        h(2, chips, rows, f_n),
        v(nd, 1, t_n),
        v(nd, 2, t_n),
        v(nd, ne, 128),
        v(nd, 1, t_n),
        v(ne, 2, f_n),
        v(ne, n_state, f_n),
        v(ne, n_state, f_n),
        v(ne, n_state, f_n),
        v(ne, 1, 128),
        v(ne, ne, f_n),
        h(ne, pad, f_n),
        h(ne, pad, f_n),
        h(ne, pad, f_n),
        h(ne, pad, f_n),
        v(ne, 1, 128),
        v(ne, 1, 128),
        v(ne, 1, 128),
        v(ne, 1, 128),
        h(2, ne, pad, f_n),
        h(2, ne, pad, f_n),
        v(heads, t_n, t_n),
        v(heads, t_n, t_n),
        pltpu.SemaphoreType.DMA((8,)),
        pltpu.SemaphoreType.DMA((2, 4, chips)),
        pltpu.SemaphoreType.DMA((2, 2, chips)),
        pltpu.SemaphoreType.DMA((2, 2, chips)),
        pltpu.SemaphoreType.DMA((4, 2, nd)),
        pltpu.SemaphoreType.DMA((12, 2, ne)),
    ]
    wide = shape((nd, rows, f_n), BF16)
    tall = shape((units, rows), BF16)
    made = pl.pallas_call(
        functools.partial(block_kernel, (nd, ne, t_n, f_n, d_all, cap)),
        out_shape=[
            shape((t_n, f_n), BF16),
            shape((t_n, f_n), BF16),
            shape((ne, f_n), F32),
            shape((1, 128), F32),
            wide,
            wide,
            tall,
            tall,
            tall,
        ],
        in_specs=[vmem] * 5 + [smem] * 2 + [vmem] * 2 + [hbm] * 3,
        out_specs=[vmem] * 4 + [hbm] * 5,
        scratch_shapes=scratch,
        compiler_params=pltpu.CompilerParams(
            collective_id=0, has_side_effects=True, vmem_limit_bytes=44 * 1024 * 1024
        ),
        name="block",
    )(
        tokens,
        routes.T,
        dt_raw.T,
        b_proj.T,
        c_proj.T,
        decay_rate,
        skip_gain,
        router_weight.T,
        out_grad,
        gate_weight[0].T,
        up_weight[0].T,
        down_weight[0],
    )
    block_out, token_grad, router_grad, small, u_rows, g_rows, gt, ut, ht = made
    two = pl.BlockSpec((2, rows, f_n), lambda j: (j, 0, 0))
    whole = pl.BlockSpec((units, rows), lambda j: (0, 0))
    span = pl.BlockSpec((units, 2 * f_n), lambda j: (0, j))
    gate_grad, up_grad, down_grad = pl.pallas_call(
        grads_kernel,
        grid=(chips,),
        out_shape=[shape((units, d_all), BF16)] * 3,
        in_specs=[two, two, whole, whole, whole],
        out_specs=[span] * 3,
        name="grads",
    )(u_rows, g_rows, gt, ut, ht)
    return (
        block_out,
        token_grad,
        gate_grad.T[None],
        up_grad.T[None],
        down_grad[None],
        router_grad.T,
        small[0, :heads],
        small[0, heads : 2 * heads],
    )


def solution(mesh):
    return jax.shard_map(
        body,
        mesh=mesh,
        in_specs=(
            P("expert", "dp"),
            P("expert", None),
            P("expert", "dp"),
            P("expert", None),
            P("expert", None),
            P("dp"),
            P("dp"),
            P("dp", None),
            P("expert", None, "dp"),
            P("expert", None, "dp"),
            P("expert", "dp", None),
            P("expert", "dp"),
        ),
        out_specs=(
            P("expert", "dp"),
            P("expert", "dp"),
            P("expert", None, "dp"),
            P("expert", None, "dp"),
            P("expert", "dp", None),
            P("dp", None),
            P("dp"),
            P("dp"),
        ),
        check_vma=False,
    )
```

time: 303 us -> 131 us (0.43)
  Pallas kernels: 0 us -> 112 us
  waiting for transfers between devices: 97.8 us -> 0 us
  starting transfers between devices: 74.4 us -> 0 us
  blocking collectives: 48.6 us -> 0 us
  matrix products: 31.7 us -> 0 us
  other arithmetic: 17.1 us -> 0 us
  local copies, waits for them, and re-layouts: 28.7 us -> 17.5 us
    pallas_call x0 -> x2, Pallas kernels: none -> 112 us  [the longest x1 104 us: body(): pl.pallas_call(functools.partial(block_kernel, (nd, ne, t_n, f_n, d_all,...]
    all_to_all x14 -> x0, waiting for transfers between devices: 97.8 us -> none  [the longest x10 58.6 us: sent_to_all(): lax.all_to_all(jnp.broadcast_to(x[None], (peers, *x.shape)), axis, 0, 0,...]
    all_to_all x14 -> x0, starting transfers between devices: 74.4 us -> none  [the longest x10 58.2 us: sent_to_all(): lax.all_to_all(jnp.broadcast_to(x[None], (peers, *x.shape)), axis, 0, 0,...]
    all_to_all x3 -> x0, blocking collectives: 48.6 us -> none  [the longest x2 25.6 us: to_units(): lax.all_to_all(send_rows, 'expert', split_axis=0, concat_axis=0, tiled=True)]
    dot_general x32 -> x0, matrix products: 31.7 us -> none  [the longest x1 3.86 us: body(): lax.dot_general(unit_rows, up_back, (((0,), (0,)), ((), ())), preferred_e...]
    unnamed x160 -> x37, local copies, waits for them, and re-layouts: 6.34 us -> 16.9 us
    broadcast_in_dim x14 -> x0, local copies, waits for them, and re-layouts: 7.57 us -> none  [the longest x13 7.53 us: sent_to_all(): jnp.broadcast_to(x[None], (peers, *x.shape))]
    reshape x14 -> x0, local copies, waits for them, and re-layouts: 6.85 us -> none  [the longest x2 2.79 us: split_up(): x.reshape(*lengths[:dim], peers, lengths[dim] // peers, *lengths[dim + 1:])]
  transfers between devices with their start and end apart: 14 -> 0, of which waited for: 14 -> 0; matrix products, arithmetic and copies ran while one was open for 13% -> 0% of each run, Pallas kernels for 0% -> 0%
where the time goes in v1:
time: 131 us; the launch traced here: 130 us
  Pallas kernels  112 us (85%)
  local copies, waits for them, and re-layouts  17.5 us (13%)
    pallas_call x1, Pallas kernels, body(): pl.pallas_call(functools.partial(block_kernel, (nd, ne, t_n, f_n, d_all,...  104 us
    unnamed x37, local copies, waits for them, and re-layouts  16.9 us
    pallas_call x1, Pallas kernels, body(): pl.pallas_call(grads_kernel, grid=(chips,), out_shape=[shape((units, d_al...  8.38 us

profile of v1, /device:TPU:1, one launch (start us, length us, event | category | flops | bytes accessed | tf_op | source)
XLA Modules:
  0.0 130.5 jit_solution(14120570644293078429)
XLA Ops:
  0.6 0.0 copy-start
  0.6 1.5 %copy-done = bf16[1,2048,448]{1,2,0:T(8,128)(2,1)S(1)} copy-done((bf16[1,2048,448]{1,2,0:T(8,128)(2,1)S(1)}, bf16[1,2048,448]{1,2,0:T(8,128)(2,1)}, u32[]{:S(2)}) %copy-start) | copy-done | bytes 1835032
  2.1 0.0 copy-start.1
  2.1 1.5 %copy-done.1 = bf16[1,2048,448]{1,2,0:T(8,128)(2,1)S(1)} copy-done((bf16[1,2048,448]{1,2,0:T(8,128)(2,1)S(1)}, bf16[1,2048,448]{1,2,0:T(8,128)(2,1)}, u32[]{:S(2)}) %copy-start.1) | copy-done | bytes 1835032
  3.6 0.0 copy-start.2
  3.6 1.5 %copy-done.2 = bf16[1,448,2048]{2,1,0:T(8,128)(2,1)S(1)} copy-done((bf16[1,448,2048]{2,1,0:T(8,128)(2,1)S(1)}, bf16[1,448,2048]{2,1,0:T(8,128)(2,1)}, u32[]{:S(2)}) %copy-start.2) | copy-done | bytes 1835032
  5.1 0.0 copy-start.8
  5.1 0.8 copy-done.8
  5.9 0.0 copy-start.9
  5.9 0.8 copy-done.9
  6.7 0.0 copy-start.10
  6.7 0.7 copy-done.10
  7.4 0.0 copy-start.11
  7.4 0.7 copy-done.11
  8.1 0.0 copy-start.12
  8.1 0.7 copy-done.12
  8.7 0.7 copy-done.13
  9.4 0.7 copy-done.14
  10.1 0.7 copy-done.15
  10.8 0.7 copy-done.16
  11.4 103.9 %block.1 = (bf16[128,128]{1,0:T(8,128)(2,1)S(1)}, bf16[128,128]{1,0:T(8,128)(2,1)S(1)}, f32[16,128]{1,0:T(8,128)S(1)}, f32[1,128]{1,0:T(1,128)S(1)}, bf16[16,320...) custom-call(bf16[128,128]{1,0:T(8,128)(2,1)S(1)} %copy-done.8, ...), custom_call_target="tpu_custom_call" | custom-call | tf_op jit(solution)/shard_map/block/pallas_call | solution.py:756
  115.3 0.0 copy-start.3
  115.3 1.1 copy-done.3
  116.4 1.1 copy-done.4
  117.5 0.7 copy-done.5
  118.2 0.7 copy-done.6
  119.0 0.7 copy-done.7
  119.7 8.4 %grads.1 = (bf16[448,2048]{1,0:T(8,128)(2,1)}, bf16[448,2048]{1,0:T(8,128)(2,1)}, bf16[448,2048]{1,0:T(8,128)(2,1)}) custom-call(bf16[16,320,128]{2,1,0:T(8,128)(2,1)} %copy-done.3, bf16[16,320,128]{2,1,0:T(8,128)(2,1)} %copy-done.4, bf16[448,320]{1,0:T(8,128)(2,1)} %copy-done.5, bf16[448,320]{1,0:T(8,128)(2,1)} %copy-done.6, bf16[448,320]{1,0:T(8,128)(2,1)} %copy-done.7), custom_call_target="tpu_custom_call" | custom-call | tf_op jit(solution)/shard_map/grads/pallas_call | solution.py:794
  128.1 0.6 slice_bitcast_fusion
  128.6 0.6 copy.23
  129.3 0.6 copy.24
  129.9 0.6 copy.25
  (8 shorter events, 0.0 us)
Async XLA Ops:
  0.6 1.5 %copy-start = (bf16[1,2048,448]{1,2,0:T(8,128)(2,1)S(1)}, bf16[1,2048,448]{1,2,0:T(8,128)(2,1)}, u32[]{:S(2)}) copy-start(bf16[1,2048,448]{1,2,0:T(8,128)(2,1)} %param.20) | copy-start | bytes 5505028
  2.1 1.5 %copy-start.1 = (bf16[1,2048,448]{1,2,0:T(8,128)(2,1)S(1)}, bf16[1,2048,448]{1,2,0:T(8,128)(2,1)}, u32[]{:S(2)}) copy-start(bf16[1,2048,448]{1,2,0:T(8,128)(2,1)} %param.21) | copy-start | bytes 5505028
  3.6 1.5 %copy-start.2 = (bf16[1,448,2048]{2,1,0:T(8,128)(2,1)S(1)}, bf16[1,448,2048]{2,1,0:T(8,128)(2,1)}, u32[]{:S(2)}) copy-start(bf16[1,448,2048]{2,1,0:T(8,128)(2,1)} %param.22) | copy-start | bytes 5505028
  5.1 0.8 copy-start.8
  5.9 0.8 copy-start.9
  6.7 0.7 copy-start.10
  7.4 0.7 copy-start.11
  8.1 0.7 copy-start.12
  8.7 0.7 copy-start.13
  9.4 0.7 copy-start.14
  10.1 0.7 copy-start.15
  10.8 0.7 copy-start.16
  115.3 1.1 copy-start.3
  116.4 1.1 copy-start.4
  117.5 0.7 copy-start.5
  118.2 0.7 copy-start.6
  118.9 0.7 copy-start.7

commit v2 on v1

--- a/solution.py
+++ b/solution.py
@@ -9,7 +9,7 @@
 
 EPSILON = 1e-06
 CAPACITY = 20
-SLOT_PAD = 32
+SLOT_PAD = 24
 HIGH = lax.Precision.HIGHEST
 F32 = jnp.float32
 BF16 = jnp.bfloat16
@@ -38,46 +38,79 @@
 
 
 class Exchange:
-    def __init__(self, axis, me, size, src, dst, sems, same=False):
+    def __init__(self, axis, me, size, src, dst, sems, width=None):
         self.axis, self.me, self.size = axis, me, size
-        self.src, self.dst, self.sems, self.same = src, dst, sems, same
+        self.src, self.dst, self.sems, self.width = src, dst, sems, width
+
+    def part(self, ref, spot):
+        if self.width is None:
+            return ref.at[spot]
+        return ref.at[spot, pl.ds(0, self.width)]
 
     def copy(self, peer):
-        src = self.dst.at[self.me] if self.same else self.src.at[peer]
+        src = self.part(self.dst, self.me) if self.src is None else self.part(self.src, peer)
         return remote(
-            src, self.dst.at[self.me], self.sems.at[0, peer], self.sems.at[1, self.me], self.axis, peer
+            src, self.part(self.dst, self.me), self.sems.at[0], self.sems.at[1], self.axis, peer
         )
 
-    def arrival(self, peer):
+    def start(self):
+        def step(k, carry):
+            self.copy(lax.rem(self.me + k, self.size)).start()
+            return carry
+
+        lax.fori_loop(1, self.size, step, 0)
+
+    def all_blocks(self):
+        span = self.part(self.dst, pl.ds(0, self.size - 1))
+        peer = lax.rem(self.me + 1, self.size)
+        return remote(span, span, self.sems.at[0], self.sems.at[1], self.axis, peer)
+
+    def wait(self):
+        self.all_blocks().wait_recv()
+
+    def drain(self):
+        self.all_blocks().wait_send()
+
+
+class Chain:
+    def __init__(self, axis, me, size, dst, sems, later):
+        self.axis, self.me, self.dst, self.sems = axis, me, dst, sems
+        self.low, self.high = (me + 1, size) if later else (0, me)
+
+    def copy(self, peer):
+        spot = self.dst.at[self.me]
+        return remote(spot, spot, self.sems.at[0, peer], self.sems.at[1, self.me], self.axis, peer)
+
+    def each(self, act):
+        def step(p, carry):
+            act(self.copy(p))
+            return carry
+
+        lax.fori_loop(self.low, self.high, step, 0)
+
+    def start(self):
+        self.each(lambda copy: copy.start())
+
+    def drain(self):
+        self.each(lambda copy: copy.wait_send())
+
+    def wait_for(self, peer):
         spot = self.dst.at[peer]
-        return remote(spot, spot, self.sems.at[0, peer], self.sems.at[1, peer], self.axis, peer)
-
-    def each(self, act, low=None, high=None):
-        if low is None:
-            def step(k, carry):
-                act(lax.rem(self.me + k, self.size))
-                return carry
-
-            lax.fori_loop(1, self.size, step, 0)
-        else:
-            def step(p, carry):
-                act(p)
-                return carry
-
-            lax.fori_loop(low, high, step, 0)
-
-    def start(self, low=None, high=None):
-        self.each(lambda p: self.copy(p).start(), low, high)
-
-    def wait(self, low=None, high=None):
-        self.each(lambda p: self.arrival(p).wait_recv(), low, high)
-
-    def drain(self, low=None, high=None):
-        self.each(lambda p: self.copy(p).wait_send(), low, high)
+        remote(spot, spot, self.sems.at[0, peer], self.sems.at[1, peer], self.axis, peer).wait_recv()
 
 
 def block_kernel(
     dims,
+    *refs,
+):
+    inputs, outputs, rest = refs[:12], refs[12:19], refs[19:]
+    loaded, scratch = rest[:9], rest[9:]
+    block_phases(dims, inputs, *loaded, *inputs[9:], *outputs, *scratch)
+
+
+def block_phases(
+    dims,
+    inputs,
     x_ref,
     routes_ref,
     dt_ref,
@@ -94,11 +127,9 @@
     token_ref,
     router_ref,
     small_ref,
-    u_hbm,
-    g_hbm,
-    gt_hbm,
-    ut_hbm,
-    ht_hbm,
+    gate_ref,
+    up_ref,
+    down_ref,
     wg,
     wu,
     wd,
@@ -149,7 +180,7 @@
     ag_sem,
     pair_sem,
     rs_sem,
-    sem_d,
+    sem_x,
     sem_e,
 ):
     nd, ne, t_n, f_n, d_all, cap = dims
@@ -175,6 +206,13 @@
     def chip_before(i):
         return lax.rem(chip_x + nx - i // ny, nx) * ny + lax.rem(chip_y + ny - lax.rem(i, ny), ny)
 
+    loaded = (x_ref, routes_ref, dt_ref, b_ref, c_ref, rate_ref, skip_ref, rw_ref, og_ref)
+    small_copies = [
+        pltpu.make_async_copy(src, dst, local_sem.at[3 + k])
+        for k, (src, dst) in enumerate(zip(inputs, loaded))
+    ]
+    for copy in small_copies:
+        copy.start()
     weight_copies = [
         pltpu.make_async_copy(src, dst, local_sem.at[k])
         for k, (src, dst) in enumerate(((wd_hbm, wd), (wg_hbm, wg), (wu_hbm, wu)))
@@ -197,20 +235,31 @@
     greet("expert", me_e, ne)
 
     def on_dp(dst, k):
-        return Exchange("dp", me_d, nd, None, dst, sem_d.at[k], same=True)
+        return Exchange("dp", me_d, nd, None, dst, sem_x.at[k])
 
     def on_expert(dst, k, src=None):
-        return Exchange("expert", me_e, ne, src, dst, sem_e.at[k], same=src is None)
+        return Exchange("expert", me_e, ne, src, dst, sem_x.at[k])
 
     ex_ar1, ex_ar2, ex_ar3, ex_ar4 = (on_dp(r, k) for k, r in enumerate((ar1, ar2, ar3, ar4)))
-    ex_dec, ex_st, ex_dl, ex_sg, ex_tot, ex_rout = (
-        on_expert(r, k) for k, r in enumerate((dec, st, dl, sg, tot, rout))
-    )
-    ex_og = on_expert(og_in, 6, og_out)
-    ex_xs = on_expert(xs_in, 7, xs_out)
-    ex_sq = on_expert(sq_in, 8, sq_out)
-    ex_sb = on_expert(sb_in, 9, sb_out)
-    ex_bk = [on_expert(bk_in.at[k], 10 + k, bk_out.at[k]) for k in range(2)]
+    ex_dec, ex_tot, ex_rout = (on_expert(r, 4 + k) for k, r in enumerate((dec, tot, rout)))
+    ex_og = on_expert(og_in, 7, og_out)
+    ex_xs = on_expert(xs_in, 8, xs_out)
+    ex_sq = on_expert(sq_in, 9, sq_out)
+    ex_sb = on_expert(sb_in, 10, sb_out)
+    ex_bk = [on_expert(bk_in.at[k], 11 + k, bk_out.at[k]) for k in range(2)]
+    ex_st, ex_dl, ex_sg = (
+        Chain("expert", me_e, ne, r, sem_e.at[k], k < 2) for k, r in enumerate((st, dl, sg))
+    )
+
+    for copy in small_copies:
+        copy.wait()
+
+    def to_blocks(ref, value):
+        for e in range(ne):
+            ref[e] = value[e * pad : (e + 1) * pad].astype(BF16)
+
+    def from_blocks(ref):
+        return jnp.concatenate([ref[e].astype(F32) for e in range(ne)], axis=0).astype(BF16)
 
     x_t = x_ref[...].astype(F32).T
     ar1[me_d] = jnp.sum(x_t * x_t, axis=0, keepdims=True)
@@ -242,7 +291,7 @@
     pick_b = jnp.where(here, mm(spread_rows, hot_b.astype(BF16)), 0.0)
     pick = (pick_a + pick_b).astype(BF16)
     og = og_ref[...]
-    og_out[...] = mm(pick, og).astype(BF16).reshape(ne, pad, f_n)
+    to_blocks(og_out, mm(pick, og))
     og_in[me_e] = og_out[me_e]
 
     pl.semaphore_wait(barrier, nd + ne - 2)
@@ -284,9 +333,8 @@
     scale_one = lax.rsqrt(jnp.sum(ar1[...], axis=0) / d_all + EPSILON)
     normed = x_t * scale_one
     st[me_e] = mm(b_rows, normed * tail, NT, HIGH)
-    ex_st.start(me_e + 1, ne)
+    ex_st.start()
     dl[me_e] = mm(b_rows, normed * tail * reach, NT, HIGH)
-    ex_dl.start(me_e + 1, ne)
     mixed = jnp.concatenate(
         [mm(normed[h * hp : (h + 1) * hp], mt[h], NN, HIGH) for h in range(heads)], axis=0
     )
@@ -330,28 +378,32 @@
         ).wait_send()
         lax.fori_loop(1, chips, step, 0)
 
-    def ag_consume(buf, k, use):
+    def ag_forwards(buf, k, low, high):
         def step(i, carry):
-            @pl.when(i < chips)
-            def _():
-                ag_forward(buf, k, i)
-
-            ag_partner(buf, k, i - 1)
-            j = chip_before(i - 1)
-            both = jnp.concatenate([buf[2 * j], buf[2 * j + 1]], axis=1)
-            use(both, pl.ds(pl.multiple_of(j * 2 * f_n, 2 * f_n), 2 * f_n))
+            ag_forward(buf, k, i)
             return carry
 
-        lax.fori_loop(1, chips + 1, step, 0)
+        lax.fori_loop(low, high, step, 0)
+
+    def ag_partners(buf, k, low, high):
+        def step(i, carry):
+            ag_partner(buf, k, i)
+            return carry
+
+        lax.fori_loop(low, high, step, 0)
+
+    def ag_chips(buf, low, high):
+        places = [chip_before(i) for i in range(low, high)]
+        rows_of = jnp.concatenate([buf[2 * j + c] for j in places for c in range(2)], axis=1)
+        return [pl.ds(pl.multiple_of(j * 2 * f_n, 2 * f_n), 2 * f_n) for j in places], rows_of
 
     ex_og.wait()
-    rows_g[me_d] = mm(compact, og_in[...].reshape(spots, f_n)).astype(BF16)
-    ag_begin(rows_g, 0)
+    rows_g[me_d] = mm(compact, from_blocks(og_in)).astype(BF16)
 
     ex_dec.wait()
 
     def carry_state(j, state):
-        ex_st.arrival(j).wait_recv()
+        ex_st.wait_for(j)
         return dec[j][0:1] * state + st[j]
 
     state_in = lax.fori_loop(0, me_e, carry_state, jnp.zeros((n_state, f_n), F32))
@@ -370,22 +422,12 @@
         axis=0,
     )
     ex_ar2.start()
-    xs_out[...] = mm(pick, resid).astype(BF16).reshape(ne, pad, f_n)
+    to_blocks(xs_out, mm(pick, resid))
     xs_in[me_e] = xs_out[me_e]
     ex_xs.start()
 
-    def carry_slope(j, both):
-        state, slope = both
-        ex_dl.arrival(j).wait_recv()
-        here_dec = dec[j]
-        return (
-            here_dec[0:1] * state + st[j],
-            here_dec[0:1] * slope + here_dec[1:2] * state + dl[j],
-        )
-
-    zero_state = jnp.zeros((n_state, f_n), F32)
-    slope_in = lax.fori_loop(0, me_e, carry_slope, (zero_state, zero_state))[1]
-
+    ag_begin(rows_g, 0)
+    ex_dl.start()
     ex_ar2.wait()
     sums = jnp.sum(ar2[...], axis=0)
     scale_two = lax.rsqrt(sums[0:1] / d_all + EPSILON)
@@ -406,21 +448,11 @@
     sq_in[me_e] = sq_out[me_e]
     ex_sq.start()
 
+    ex_xs.wait()
+    rows_u[me_d] = mm(compact, from_blocks(xs_in)).astype(BF16)
+    ag_begin(rows_u, 1)
+    ag_forwards(rows_g, 0, 1, chips)
     weight_copies[0].wait()
-    vacc[...] = jnp.zeros_like(vacc)
-
-    def use_grad(both, span):
-        vacc[...] += mm(both, wd[:, span], NT)
-
-    ag_consume(rows_g, 0, use_grad)
-
-    ex_xs.wait()
-    rows_u[me_d] = mm(compact, xs_in[...].reshape(spots, f_n)).astype(BF16)
-    ag_begin(rows_u, 1)
-    weight_copies[1].wait()
-    weight_copies[2].wait()
-    gacc[...] = jnp.zeros_like(gacc)
-    uacc[...] = jnp.zeros_like(uacc)
     ex_sq.wait()
 
     def by_row(ref):
@@ -430,19 +462,22 @@
     wide = by_row(sq_in)
     cols[0] = jnp.sum(jnp.where(lane_first, wide, 0.0), axis=1, keepdims=True)
     cols[1] = jnp.sum(jnp.where(lane_second, wide, 0.0), axis=1, keepdims=True)
-
-    def use_rows(both, span):
-        gacc[...] += mm(both, wg[:, span], NT)
-        uacc[...] += mm(both, wu[:, span], NT)
-
-    ag_consume(rows_u, 1, use_rows)
-    out_copies = [
-        pltpu.make_async_copy(rows_g, g_hbm, local_sem.at[3]),
-        pltpu.make_async_copy(rows_u, u_hbm, local_sem.at[4]),
-    ]
-    for copy in out_copies:
-        copy.start()
-
+    ag_partners(rows_g, 0, 0, chips)
+    vacc[...] = mm(jnp.concatenate([rows_g[d] for d in range(nd)], axis=1), wd[...], NT)
+    weight_copies[1].wait()
+    weight_copies[2].wait()
+    half = chips // 2
+    more = min(chips, half + 2)
+    ag_forwards(rows_u, 1, 1, more)
+    ag_partners(rows_u, 1, 0, half)
+    spans, both = ag_chips(rows_u, 0, half)
+    gacc[...] = mm(both, jnp.concatenate([wg[:, span] for span in spans], axis=1), NT)
+    uacc[...] = mm(both, jnp.concatenate([wu[:, span] for span in spans], axis=1), NT)
+    ag_forwards(rows_u, 1, more, chips)
+    ag_partners(rows_u, 1, half, chips)
+    spans, both = ag_chips(rows_u, half, chips)
+    gacc[...] += mm(both, jnp.concatenate([wg[:, span] for span in spans], axis=1), NT)
+    uacc[...] += mm(both, jnp.concatenate([wu[:, span] for span in spans], axis=1), NT)
     part = rows // 5
 
     def units(k, carry):
@@ -477,39 +512,6 @@
     ar3[me_d] = mm(of_block_t, zrow[...], NN, HIGH)
     ex_ar3.start()
 
-    def rs_pass(k, terms):
-        def finish(i):
-            j = chip_after(i)
-            remote(
-                pair_in.at[k, j], pair_in.at[k, j], pair_sem.at[k, 0, j], pair_sem.at[k, 1, j], "dp", partner
-            ).wait_recv()
-            total = keep[k, j] + pair_in[k, j].astype(F32)
-            rs_out[k, i] = total.astype(BF16)
-
-            @pl.when(i > 0)
-            def _():
-                rs_copy(k, i).start()
-
-        def step(n, carry):
-            @pl.when(n < chips)
-            def _():
-                i = lax.rem(n + 1, chips)
-                j = chip_after(i)
-                both = terms(pl.ds(pl.multiple_of(j * 2 * f_n, 2 * f_n), 2 * f_n))
-                low, high = both[:, :f_n], both[:, f_n:]
-                first = core == 0
-                keep[k, j] = jnp.where(first, low, high)
-                pair_out[k, j] = jnp.where(first, high, low).astype(BF16)
-                pair_copy(k, j).start()
-
-            @pl.when(n > 0)
-            def _():
-                finish(lax.rem(n, chips))
-
-            return carry
-
-        lax.fori_loop(0, chips + 1, step, 0)
-
     def pair_copy(k, j):
         return remote(
             pair_out.at[k, j], pair_in.at[k, j], pair_sem.at[k, 0, j], pair_sem.at[k, 1, j], "dp", partner
@@ -520,8 +522,47 @@
             rs_out.at[k, i], rs_in.at[k, i], rs_sem.at[k, 0, i], rs_sem.at[k, 1, i], "dp", chip_after(i) * 2 + core
         )
 
-    rs_pass(0, lambda span: mm(hid[...], wd[:, span]))
-    rs_pass(1, lambda span: mm(gb[...], wg[:, span]) + mm(ub[...], wu[:, span]))
+    def rs_terms(k, n, terms):
+        j = chip_after(lax.rem(n + 1, chips))
+        both = terms(pl.ds(pl.multiple_of(j * 2 * f_n, 2 * f_n), 2 * f_n))
+        low, high = both[:, :f_n], both[:, f_n:]
+        first = core == 0
+        keep[k, j] = jnp.where(first, low, high)
+        pair_out[k, j] = jnp.where(first, high, low).astype(BF16)
+        pair_copy(k, j).start()
+
+    def rs_send(m):
+        k, i = m // chips, lax.rem(m + 1, chips)
+        j = chip_after(i)
+        remote(
+            pair_in.at[k, j], pair_in.at[k, j], pair_sem.at[k, 0, j], pair_sem.at[k, 1, j], "dp", partner
+        ).wait_recv()
+        rs_out[k, i] = (keep[k, j] + pair_in[k, j].astype(F32)).astype(BF16)
+
+        @pl.when(i > 0)
+        def _():
+            rs_copy(k, i).start()
+
+    lag = 3
+
+    def rs_step(n, carry):
+        @pl.when(n < chips)
+        def _():
+            rs_terms(0, n, lambda span: mm(hid[...], wd[:, span]))
+
+        @pl.when((n >= chips) & (n < 2 * chips))
+        def _():
+            rs_terms(
+                1, n - chips, lambda span: mm(gb[...], wg[:, span]) + mm(ub[...], wu[:, span])
+            )
+
+        @pl.when(n >= lag)
+        def _():
+            rs_send(n - lag)
+
+        return carry
+
+    lax.fori_loop(0, 2 * chips + lag, rs_step, 0)
 
     ex_ar3.wait()
     line = jnp.sum(ar3[...], axis=0)
@@ -530,11 +571,19 @@
     sb_in[me_e] = sb_out[me_e]
     ex_sb.start()
 
-    for k, (src, dst, out) in enumerate(((gs, gst, gt_hbm), (us, ust, ut_hbm), (hs, hst, ht_hbm))):
+    for src, dst in ((gs, gst), (us, ust), (hs, hst)):
         dst[...] = src[...].T.astype(BF16)
-        copy = pltpu.make_async_copy(dst, out, local_sem.at[5 + k])
-        copy.start()
-        out_copies.append(copy)
+
+    def weight_grads(j, carry):
+        span = pl.ds(pl.multiple_of(j * 2 * f_n, 2 * f_n), 2 * f_n)
+        both_u = jnp.concatenate([rows_u[2 * j], rows_u[2 * j + 1]], axis=1)
+        both_g = jnp.concatenate([rows_g[2 * j], rows_g[2 * j + 1]], axis=1)
+        gate_ref[:, span] = mm(gst[...], both_u).astype(BF16)
+        up_ref[:, span] = mm(ust[...], both_u).astype(BF16)
+        down_ref[:, span] = mm(hst[...], both_g).astype(BF16)
+        return carry
+
+    lax.fori_loop(0, chips, weight_grads, 0)
 
     def rs_finish(k):
         def step(i, total):
@@ -547,12 +596,13 @@
         wide_rows = lax.dot_general(
             compact, total.astype(BF16), (((0,), (0,)), ((), ())), preferred_element_type=F32
         )
-        bk_out[k] = wide_rows.astype(BF16).reshape(ne, pad, f_n)
+        to_blocks(bk_out.at[k], wide_rows)
         bk_in[k, me_e] = bk_out[k, me_e]
         ex_bk[k].start()
 
     rs_finish(0)
 
+    rs_finish(1)
     ex_sb.wait()
     table = jnp.concatenate([sb_in[e] for e in range(ne)], axis=0)
     by_spot = mm(spread_rows.astype(F32), table, NN, HIGH)
@@ -572,20 +622,49 @@
     first_m = jnp.broadcast_to(first_w, (f_n, t_n)).T
     second_m = jnp.broadcast_to(second_w, (f_n, t_n)).T
 
-    rs_finish(1)
+    def carry_slope(j, both):
+        state, slope = both
+        ex_dl.wait_for(j)
+        here_dec = dec[j]
+        return (
+            here_dec[0:1] * state + st[j],
+            here_dec[0:1] * slope + here_dec[1:2] * state + dl[j],
+        )
+
+    zero_state = jnp.zeros((n_state, f_n), F32)
+    slope_in = lax.fori_loop(0, me_e, carry_slope, (zero_state, zero_state))[1]
+
+    for ex in (ex_ar1, ex_ar2, ex_ar3, ex_dec, ex_og, ex_xs, ex_sq):
+        ex.drain()
+    ex_st.drain()
+    ex_dl.drain()
+    ag_drain(rows_g, 0)
+    ag_drain(rows_u, 1)
+    for k in range(2):
+        def step(i, carry, k=k):
+            pair_copy(k, i).wait_send()
+
+            @pl.when(i > 0)
+            def _():
+                rs_copy(k, i).wait_send()
+
+            return carry
+
+        lax.fori_loop(0, chips, step, 0)
+
     ex_bk[0].wait()
-    came = bk_in[0].reshape(spots, f_n)
+    came = from_blocks(bk_in.at[0])
     block_ref[...] = (
         resid.astype(F32) + (first_m * mm(pick_at, came) + second_m * mm(pick_bt, came))
     ).astype(BF16)
 
     ex_bk[1].wait()
-    moe_grad = mm(pick_at + pick_bt, bk_in[1].reshape(spots, f_n)).T
+    moe_grad = mm(pick_at + pick_bt, from_blocks(bk_in.at[1])).T
     grad = resid_base + scale_two * moe_grad
     state_grads = [mm(c_rows * fades[h], grad, NT, HIGH) for h in range(heads)]
     state_grad = jnp.where(head_lane, state_grads[0], state_grads[1])
     sg[me_e] = state_grad
-    ex_sg.start(0, me_e)
+    ex_sg.start()
 
     normed_rows = normed.T
     cum_f = jnp.where(head_row, cum[0:1], cum[1:2])
@@ -617,7 +696,7 @@
 
     def carry_grad(n, later):
         j = ne - 1 - n
-        ex_sg.arrival(j).wait_recv()
+        ex_sg.wait_for(j)
         return dec[j][0:1] * later + sg[j]
 
     later = lax.fori_loop(0, ne - 1 - me_e, carry_grad, zero_state)
@@ -635,34 +714,22 @@
     ex_tot.wait()
     small_ref[...] = jnp.sum(tot[...], axis=0)
 
-    for ex in (ex_ar1, ex_ar2, ex_ar3, ex_ar4, ex_dec, ex_tot, ex_rout, ex_og, ex_xs, ex_sq, ex_sb, *ex_bk):
+    for ex in (ex_ar4, ex_tot, ex_rout, ex_sb, *ex_bk):
         ex.drain()
-    ex_st.drain(me_e + 1, ne)
-    ex_dl.drain(me_e + 1, ne)
-    ex_sg.drain(0, me_e)
-    ag_drain(rows_g, 0)
-    ag_drain(rows_u, 1)
-    for k in range(2):
-        def step(i, carry, k=k):
-            pair_copy(k, i).wait_send()
-
-            @pl.when(i > 0)
-            def _():
-                rs_copy(k, i).wait_send()
-
-            return carry
-
-        lax.fori_loop(0, chips, step, 0)
-    for copy in out_copies:
+    ex_sg.drain()
+
+
+def flush_kernel(*refs):
+    made, small_ref, outs, sem = refs[:6], refs[6], refs[7:13], refs[15]
+    copies = [pltpu.make_async_copy(a, b, sem.at[k]) for k, (a, b) in enumerate(zip(made, outs))]
+    for copy in copies:
+        copy.start()
+    rate_ref, skip_ref = refs[13], refs[14]
+    heads = rate_ref.shape[0]
+    rate_ref[...] = small_ref[0, 0:heads]
+    skip_ref[...] = small_ref[0, heads : 2 * heads]
+    for copy in copies:
         copy.wait()
-
-
-def grads_kernel(u_ref, g_ref, gt_ref, ut_ref, ht_ref, gate_ref, up_ref, down_ref):
-    both_u = jnp.concatenate([u_ref[0], u_ref[1]], axis=1)
-    both_g = jnp.concatenate([g_ref[0], g_ref[1]], axis=1)
-    gate_ref[...] = mm(gt_ref[...], both_u).astype(BF16)
-    up_ref[...] = mm(ut_ref[...], both_u).astype(BF16)
-    down_ref[...] = mm(ht_ref[...], both_g).astype(BF16)
 
 
 def body(
@@ -686,8 +753,8 @@
     units = down_weight.shape[1]
     cap, pad = CAPACITY, SLOT_PAD
     rows, chips = ne * cap, nd // 2
-    vmem, hbm, smem = (
-        pl.BlockSpec(memory_space=space) for space in (pltpu.VMEM, pl.ANY, pltpu.SMEM)
+    vmem, hbm, anywhere = (
+        pl.BlockSpec(memory_space=space) for space in (pltpu.VMEM, pltpu.HBM, pl.ANY)
     )
     def v(*s):
         return pltpu.VMEM(s, F32)
@@ -698,6 +765,15 @@
     def shape(s, t):
         return jax.ShapeDtypeStruct(s, t)
     scratch = [
+        h(t_n, f_n),
+        pltpu.VMEM((2, t_n), jnp.int32),
+        v(heads, t_n),
+        v(n_state, t_n),
+        v(n_state, t_n),
+        pltpu.SMEM((heads,), F32),
+        pltpu.SMEM((heads,), F32),
+        v(ne, f_n),
+        h(t_n, f_n),
         h(units, d_all),
         h(units, d_all),
         h(units, d_all),
@@ -744,33 +820,31 @@
         h(2, ne, pad, f_n),
         v(heads, t_n, t_n),
         v(heads, t_n, t_n),
-        pltpu.SemaphoreType.DMA((8,)),
+        pltpu.SemaphoreType.DMA((12,)),
         pltpu.SemaphoreType.DMA((2, 4, chips)),
         pltpu.SemaphoreType.DMA((2, 2, chips)),
         pltpu.SemaphoreType.DMA((2, 2, chips)),
-        pltpu.SemaphoreType.DMA((4, 2, nd)),
-        pltpu.SemaphoreType.DMA((12, 2, ne)),
+        pltpu.SemaphoreType.DMA((13, 2)),
+        pltpu.SemaphoreType.DMA((3, 2, ne)),
     ]
-    wide = shape((nd, rows, f_n), BF16)
-    tall = shape((units, rows), BF16)
+    grad_shape = h(units, d_all)
+    token_shape = h(t_n, f_n)
     made = pl.pallas_call(
         functools.partial(block_kernel, (nd, ne, t_n, f_n, d_all, cap)),
         out_shape=[
-            shape((t_n, f_n), BF16),
-            shape((t_n, f_n), BF16),
-            shape((ne, f_n), F32),
-            shape((1, 128), F32),
-            wide,
-            wide,
-            tall,
-            tall,
-            tall,
+            token_shape,
+            token_shape,
+            v(ne, f_n),
+            v(1, 128),
+            grad_shape,
+            grad_shape,
+            grad_shape,
         ],
-        in_specs=[vmem] * 5 + [smem] * 2 + [vmem] * 2 + [hbm] * 3,
-        out_specs=[vmem] * 4 + [hbm] * 5,
+        in_specs=[hbm] * 12,
+        out_specs=[vmem] * 7,
         scratch_shapes=scratch,
         compiler_params=pltpu.CompilerParams(
-            collective_id=0, has_side_effects=True, vmem_limit_bytes=44 * 1024 * 1024
+            collective_id=0, has_side_effects=True, vmem_limit_bytes=61400000
         ),
         name="block",
     )(
@@ -787,18 +861,17 @@
         up_weight[0].T,
         down_weight[0],
     )
-    block_out, token_grad, router_grad, small, u_rows, g_rows, gt, ut, ht = made
-    two = pl.BlockSpec((2, rows, f_n), lambda j: (j, 0, 0))
-    whole = pl.BlockSpec((units, rows), lambda j: (0, 0))
-    span = pl.BlockSpec((units, 2 * f_n), lambda j: (0, j))
-    gate_grad, up_grad, down_grad = pl.pallas_call(
-        grads_kernel,
-        grid=(chips,),
-        out_shape=[shape((units, d_all), BF16)] * 3,
-        in_specs=[two, two, whole, whole, whole],
-        out_specs=[span] * 3,
-        name="grads",
-    )(u_rows, g_rows, gt, ut, ht)
+    block_out, token_grad, router_grad, small, gate_grad, up_grad, down_grad = made
+    outs = (gate_grad, up_grad, down_grad, block_out, token_grad, router_grad)
+    gate_grad, up_grad, down_grad, block_out, token_grad, router_grad, rate_grad, skip_grad = pl.pallas_call(
+        flush_kernel,
+        out_shape=[shape(a.shape, a.dtype) for a in outs] + [shape((heads,), F32)] * 2,
+        in_specs=[anywhere] * 6 + [vmem],
+        out_specs=[hbm] * 6 + [vmem] * 2,
+        scratch_shapes=[pltpu.SemaphoreType.DMA((6,))],
+        compiler_params=pltpu.CompilerParams(vmem_limit_bytes=4 * 1024 * 1024),
+        name="flush",
+    )(*outs, small)
     return (
         block_out,
         token_grad,
@@ -806,8 +879,8 @@
         up_grad.T[None],
         down_grad[None],
         router_grad.T,
-        small[0, :heads],
-        small[0, heads : 2 * heads],
+        rate_grad,
+        skip_grad,
     )
 
 

time: 131 us -> 89.8 us (0.69)
  Pallas kernels: 112 us -> 89.1 us
  local copies, waits for them, and re-layouts: 17.5 us -> 0 us
    pallas_call x1, Pallas kernels: 104 us -> 86.1 us  [body(): pl.pallas_call(functools.partial(block_kernel, (nd, ne, t_n, f_n, d_all,...]
    unnamed x37 -> x0, local copies, waits for them, and re-layouts: 16.9 us -> none
    pallas_call x1, Pallas kernels: 8.38 us -> 3.01 us  [body(): pl.pallas_call(flush_kernel, out_shape=[shape(a.shape, a.dtype) for a in...]
where the time goes in v2:
time: 89.8 us; the launch traced here: 89.7 us
  Pallas kernels  89.1 us (99%)
    pallas_call x1, Pallas kernels, body(): pl.pallas_call(functools.partial(block_kernel, (nd, ne, t_n, f_n, d_all,...  86.1 us
    pallas_call x1, Pallas kernels, body(): pl.pallas_call(flush_kernel, out_shape=[shape(a.shape, a.dtype) for a in...  3.01 us

profile of v2, /device:TPU:1, one launch (start us, length us, event | category | flops | bytes accessed | tf_op | source)
XLA Modules:
  0.0 89.7 jit_solution(9754354487133189667)
XLA Ops:
  0.6 86.1 %block.1 = (bf16[128,128]{1,0:T(8,128)(2,1)S(1)}, bf16[128,128]{1,0:T(8,128)(2,1)S(1)}, f32[16,128]{1,0:T(8,128)S(1)}, f32[1,128]{1,0:T(1,128)S(1)}, bf16[448,20...) custom-call(bf16[128,128]{1,0:T(8,128)(2,1)} %refs_0_.1, s32[2,128]{1,0:T(2,128)} %bitcast.26, ...), custom_call_target="tpu_custom_call" | custom-call | tf_op jit(solution)/shard_map/block/pallas_call | solution.py:832
  86.7 3.0 %flush.1 = (bf16[448,2048]{1,0:T(8,128)(2,1)}, bf16[448,2048]{1,0:T(8,128)(2,1)}, bf16[448,2048]{1,0:T(8,128)(2,1)}, bf16[128,128]{1,0:T(8,128)(2,1)}, bf16[128,...) custom-call(bf16[448,2048]{1,0:T(8,128)(2,1)S(1)} %get-tuple-element.23.refs_0_, ...), custom_call_target="tpu_custom_call" | custom-call | tf_op jit(solution)/shard_map/flush/pallas_call | solution.py:866

commit v3 on v2

--- a/solution.py
+++ b/solution.py
@@ -37,6 +37,12 @@
     )
 
 
+def far_first(size):
+    ring = min(8, size)
+    order = sorted(range(ring), key=lambda k: -min(k, ring - k))
+    return [base + k for base in range(size - ring, -1, -ring) for k in order if base + k]
+
+
 class Exchange:
     def __init__(self, axis, me, size, src, dst, sems, width=None):
         self.axis, self.me, self.size = axis, me, size
@@ -54,11 +60,8 @@
         )
 
     def start(self):
-        def step(k, carry):
+        for k in far_first(self.size):
             self.copy(lax.rem(self.me + k, self.size)).start()
-            return carry
-
-        lax.fori_loop(1, self.size, step, 0)
 
     def all_blocks(self):
         span = self.part(self.dst, pl.ds(0, self.size - 1))
@@ -74,19 +77,21 @@
 
 class Chain:
     def __init__(self, axis, me, size, dst, sems, later):
-        self.axis, self.me, self.dst, self.sems = axis, me, dst, sems
-        self.low, self.high = (me + 1, size) if later else (0, me)
+        self.axis, self.me, self.size, self.dst, self.sems = axis, me, size, dst, sems
+        self.later = later
 
     def copy(self, peer):
         spot = self.dst.at[self.me]
         return remote(spot, spot, self.sems.at[0, peer], self.sems.at[1, self.me], self.axis, peer)
 
     def each(self, act):
+        low, high = (self.me + 1, self.size) if self.later else (0, self.me)
+
         def step(p, carry):
             act(self.copy(p))
             return carry
 
-        lax.fori_loop(self.low, self.high, step, 0)
+        lax.fori_loop(low, high, step, 0)
 
     def start(self):
         self.each(lambda copy: copy.start())
@@ -154,6 +159,7 @@
     pair_in,
     rs_out,
     rs_in,
+    cross,
     ar1,
     ar2,
     ar3,
@@ -191,7 +197,7 @@
     rows = ne * cap
     spots = ne * pad
     chips = nd // 2
-    ny = min(4, chips)
+    ny = chips // 2
     nx = chips // ny
     me_d = lax.axis_index("dp")
     me_e = lax.axis_index("expert")
@@ -205,6 +211,17 @@
 
     def chip_before(i):
         return lax.rem(chip_x + nx - i // ny, nx) * ny + lax.rem(chip_y + ny - lax.rem(i, ny), ny)
+
+    barrier = pltpu.get_barrier_semaphore()
+
+    def greet(axis, me, size):
+        for k in far_first(size):
+            pl.semaphore_signal(
+                barrier, inc=1, device_id={axis: lax.rem(me + k, size)}, device_id_type=MESH
+            )
+
+    greet("expert", me_e, ne)
+    greet("dp", me_d, nd)
 
     loaded = (x_ref, routes_ref, dt_ref, b_ref, c_ref, rate_ref, skip_ref, rw_ref, og_ref)
     small_copies = [
@@ -219,20 +236,6 @@
     ]
     for copy in weight_copies:
         copy.start()
-
-    barrier = pltpu.get_barrier_semaphore()
-
-    def greet(axis, me, size):
-        def step(k, carry):
-            pl.semaphore_signal(
-                barrier, inc=1, device_id={axis: lax.rem(me + k, size)}, device_id_type=MESH
-            )
-            return carry
-
-        lax.fori_loop(1, size, step, 0)
-
-    greet("dp", me_d, nd)
-    greet("expert", me_e, ne)
 
     def on_dp(dst, k):
         return Exchange("dp", me_d, nd, None, dst, sem_x.at[k])
@@ -332,33 +335,48 @@
     ex_ar1.wait()
     scale_one = lax.rsqrt(jnp.sum(ar1[...], axis=0) / d_all + EPSILON)
     normed = x_t * scale_one
-    st[me_e] = mm(b_rows, normed * tail, NT, HIGH)
+    st[me_e] = mm(b_rows, normed * tail, NT, HIGH).astype(BF16)
     ex_st.start()
-    dl[me_e] = mm(b_rows, normed * tail * reach, NT, HIGH)
+    dl[me_e] = mm(b_rows, normed * tail * reach, NT, HIGH).astype(BF16)
     mixed = jnp.concatenate(
         [mm(normed[h * hp : (h + 1) * hp], mt[h], NN, HIGH) for h in range(heads)], axis=0
     )
     mixed = mixed + skip_f * normed
 
+    def ag_send(buf, k, i, spot, peer):
+        piece = buf.at[spot]
+        remote(piece, piece, ag_sem.at[k, 0, i], ag_sem.at[k, 1, i], "dp", peer * 2 + core).start()
+
     def ag_begin(buf, k):
-        def step(i, carry):
-            peer = chip_after(i) * 2 + core
-            remote(
-                buf.at[me_d], buf.at[me_d], ag_sem.at[k, 0, i], ag_sem.at[k, 1, i], "dp", peer
-            ).start()
-            return carry
-
+        for i in (2, ny, 1, 3):
+            ag_send(buf, k, i, me_d, chip_after(i))
         remote(
             buf.at[me_d], buf.at[me_d], ag_sem.at[k, 2, 0], ag_sem.at[k, 3, 0], "dp", partner
         ).start()
-        lax.fori_loop(1, chips, step, 0)
+
+    def ag_relay(buf, k):
+        spot = ag_arrived(buf, k, ny)
+        for i in (1, 3):
+            ag_send(buf, k, ny + i, spot, chip_after(i))
+        ag_pass(buf, k, ny)
+        spot = ag_arrived(buf, k, 2)
+        ag_send(buf, k, ny + 2, spot, chip_after(ny))
+        ag_pass(buf, k, 2)
+
+    def ag_arrived(buf, k, i):
+        spot = chip_before(i) * 2 + core
+        remote(
+            buf.at[spot], buf.at[spot], ag_sem.at[k, 0, i], ag_sem.at[k, 1, i], "dp", chip_before(i) * 2 + core
+        ).wait_recv()
+        return spot
+
+    def ag_pass(buf, k, i):
+        spot = buf.at[chip_before(i) * 2 + core]
+        remote(spot, spot, ag_sem.at[k, 2, i], ag_sem.at[k, 3, i], "dp", partner).start()
 
     def ag_forward(buf, k, i):
-        spot = buf.at[chip_before(i) * 2 + core]
-        remote(
-            spot, spot, ag_sem.at[k, 0, i], ag_sem.at[k, 1, i], "dp", chip_before(i) * 2 + core
-        ).wait_recv()
-        remote(spot, spot, ag_sem.at[k, 2, i], ag_sem.at[k, 3, i], "dp", partner).start()
+        ag_arrived(buf, k, i)
+        ag_pass(buf, k, i)
 
     def ag_partner(buf, k, i):
         spot = buf.at[chip_before(i) * 2 + 1 - core]
@@ -378,33 +396,36 @@
         ).wait_send()
         lax.fori_loop(1, chips, step, 0)
 
-    def ag_forwards(buf, k, low, high):
-        def step(i, carry):
+    def ag_forwards(buf, k, turns):
+        for i in turns:
             ag_forward(buf, k, i)
-            return carry
-
-        lax.fori_loop(low, high, step, 0)
-
-    def ag_partners(buf, k, low, high):
-        def step(i, carry):
+
+    def ag_partners(buf, k, turns):
+        for i in turns:
             ag_partner(buf, k, i)
-            return carry
-
-        lax.fori_loop(low, high, step, 0)
-
-    def ag_chips(buf, low, high):
-        places = [chip_before(i) for i in range(low, high)]
+
+    def ag_chips(buf, turns):
+        places = [chip_before(i) for i in turns]
         rows_of = jnp.concatenate([buf[2 * j + c] for j in places for c in range(2)], axis=1)
         return [pl.ds(pl.multiple_of(j * 2 * f_n, 2 * f_n), 2 * f_n) for j in places], rows_of
 
+    def take_rows(turns, first):
+        ag_partners(rows_u, 1, turns)
+        spans, both = ag_chips(rows_u, turns)
+        for acc, weight in ((gacc, wg), (uacc, wu)):
+            part = mm(both, jnp.concatenate([weight[:, span] for span in spans], axis=1), NT)
+            acc[...] = part if first else acc[...] + part
+
     ex_og.wait()
     rows_g[me_d] = mm(compact, from_blocks(og_in)).astype(BF16)
+    ag_begin(rows_g, 0)
 
     ex_dec.wait()
+    ag_relay(rows_g, 0)
 
     def carry_state(j, state):
         ex_st.wait_for(j)
-        return dec[j][0:1] * state + st[j]
+        return dec[j][0:1] * state + st[j].astype(F32)
 
     state_in = lax.fori_loop(0, me_e, carry_state, jnp.zeros((n_state, f_n), F32))
     state_col = state_in.T
@@ -414,6 +435,9 @@
     )
     resid_t = (x_t + (mixed + from_state)).astype(BF16).astype(F32)
     resid = resid_t.T.astype(BF16)
+    to_blocks(xs_out, mm(pick, resid))
+    xs_in[me_e] = xs_out[me_e]
+    ex_xs.start()
     ar2[me_d] = jnp.concatenate(
         [
             jnp.sum(resid_t * resid_t, axis=0, keepdims=True),
@@ -422,12 +446,8 @@
         axis=0,
     )
     ex_ar2.start()
-    to_blocks(xs_out, mm(pick, resid))
-    xs_in[me_e] = xs_out[me_e]
-    ex_xs.start()
-
-    ag_begin(rows_g, 0)
-    ex_dl.start()
+    ag_forwards(rows_g, 0, (1, 3, 5, 7, 6))
+
     ex_ar2.wait()
     sums = jnp.sum(ar2[...], axis=0)
     scale_two = lax.rsqrt(sums[0:1] / d_all + EPSILON)
@@ -451,8 +471,15 @@
     ex_xs.wait()
     rows_u[me_d] = mm(compact, from_blocks(xs_in)).astype(BF16)
     ag_begin(rows_u, 1)
-    ag_forwards(rows_g, 0, 1, chips)
     weight_copies[0].wait()
+    ag_partners(rows_g, 0, range(chips))
+    vacc[...] = mm(jnp.concatenate([rows_g[d] for d in range(nd)], axis=1), wd[...], NT)
+    weight_copies[1].wait()
+    weight_copies[2].wait()
+    ex_dl.start()
+    ag_relay(rows_u, 1)
+    ag_forwards(rows_u, 1, (1, 3))
+    take_rows((0, 1, 2, 3), True)
     ex_sq.wait()
 
     def by_row(ref):
@@ -462,22 +489,9 @@
     wide = by_row(sq_in)
     cols[0] = jnp.sum(jnp.where(lane_first, wide, 0.0), axis=1, keepdims=True)
     cols[1] = jnp.sum(jnp.where(lane_second, wide, 0.0), axis=1, keepdims=True)
-    ag_partners(rows_g, 0, 0, chips)
-    vacc[...] = mm(jnp.concatenate([rows_g[d] for d in range(nd)], axis=1), wd[...], NT)
-    weight_copies[1].wait()
-    weight_copies[2].wait()
-    half = chips // 2
-    more = min(chips, half + 2)
-    ag_forwards(rows_u, 1, 1, more)
-    ag_partners(rows_u, 1, 0, half)
-    spans, both = ag_chips(rows_u, 0, half)
-    gacc[...] = mm(both, jnp.concatenate([wg[:, span] for span in spans], axis=1), NT)
-    uacc[...] = mm(both, jnp.concatenate([wu[:, span] for span in spans], axis=1), NT)
-    ag_forwards(rows_u, 1, more, chips)
-    ag_partners(rows_u, 1, half, chips)
-    spans, both = ag_chips(rows_u, half, chips)
-    gacc[...] += mm(both, jnp.concatenate([wg[:, span] for span in spans], axis=1), NT)
-    uacc[...] += mm(both, jnp.concatenate([wu[:, span] for span in spans], axis=1), NT)
+    ag_forwards(rows_u, 1, (5, 7, 6))
+    take_rows((4, 5, 7), False)
+    take_rows((6,), False)
     part = rows // 5
 
     def units(k, carry):
@@ -485,7 +499,7 @@
         scale, weight = cols[0, span], cols[1, span]
         gate_in, up_in, grad_in = gacc[span], uacc[span], vacc[span]
         gate, up, grad = gate_in * scale, up_in * scale, grad_in * weight
-        sigma = 1.0 / (1.0 + jnp.exp(-gate))
+        sigma = 0.5 + 0.5 * jnp.tanh(0.5 * gate)
         silu = gate * sigma
         hidden = silu * up
         gate_back = grad * up * sigma * (1.0 + gate * (1.0 - sigma))
@@ -506,7 +520,7 @@
         )
         return carry
 
-    lax.fori_loop(0, 5, units, 0)
+    lax.fori_loop(0, rows // part, units, 0)
     block_t_b, block_t_r = iota((ne, rows), 0) * cap, iota((ne, rows), 1)
     of_block_t = ((block_t_r >= block_t_b) & (block_t_r < block_t_b + cap)).astype(F32)
     ar3[me_d] = mm(of_block_t, zrow[...], NN, HIGH)
@@ -519,11 +533,44 @@
 
     def rs_copy(k, i):
         return remote(
-            rs_out.at[k, i], rs_in.at[k, i], rs_sem.at[k, 0, i], rs_sem.at[k, 1, i], "dp", chip_after(i) * 2 + core
+            rs_out.at[k, i], rs_in.at[k, i], rs_sem.at[k, 0, i], rs_sem.at[k, 1, i], "dp", chip_after(lax.rem(i, ny)) * 2 + core
         )
 
+    def rs_arrival(k, i):
+        spot = rs_in.at[k, i]
+        return remote(spot, spot, rs_sem.at[k, 0, i], rs_sem.at[k, 1, i], "dp", partner)
+
+    def rs_side_copy(k):
+        return remote(
+            rs_out.at[k, ny + 2], rs_in.at[k, ny + 2], rs_sem.at[k, 0, ny + 2], rs_sem.at[k, 1, ny + 2], "dp", chip_after(ny) * 2 + core
+        )
+
+    def rs_far(k):
+        rs_arrival(k, ny + 2).wait_recv()
+        rs_out[k, 2] = (rs_out[k, 2].astype(F32) + rs_in[k, ny + 2].astype(F32)).astype(BF16)
+        rs_copy(k, 2).start()
+
+    def rs_cross(k):
+        return remote(
+            cross.at[k], rs_in.at[k, ny], rs_sem.at[k, 0, ny], rs_sem.at[k, 1, ny], "dp", chip_after(ny) * 2 + core
+        )
+
+    def rs_total(k, first, turns):
+        total = rs_out[k, first].astype(F32)
+        for i in turns:
+            rs_arrival(k, i).wait_recv()
+            total = total + rs_in[k, i].astype(F32)
+        return total
+
+    def rs_relay(k):
+        cross[k] = rs_total(k, ny, (ny + 3, ny + 1)).astype(BF16)
+        rs_cross(k).start()
+
+    def rs_index(n):
+        return (1 - n // ny) * ny + lax.rem(n + 2 + n // ny, ny)
+
     def rs_terms(k, n, terms):
-        j = chip_after(lax.rem(n + 1, chips))
+        j = chip_after(rs_index(n))
         both = terms(pl.ds(pl.multiple_of(j * 2 * f_n, 2 * f_n), 2 * f_n))
         low, high = both[:, :f_n], both[:, f_n:]
         first = core == 0
@@ -531,38 +578,54 @@
         pair_out[k, j] = jnp.where(first, high, low).astype(BF16)
         pair_copy(k, j).start()
 
-    def rs_send(m):
-        k, i = m // chips, lax.rem(m + 1, chips)
+    def rs_join(k, n):
+        i = rs_index(n)
         j = chip_after(i)
         remote(
             pair_in.at[k, j], pair_in.at[k, j], pair_sem.at[k, 0, j], pair_sem.at[k, 1, j], "dp", partner
         ).wait_recv()
         rs_out[k, i] = (keep[k, j] + pair_in[k, j].astype(F32)).astype(BF16)
-
-        @pl.when(i > 0)
+        return i
+
+    def rs_send(k, i):
+        @pl.when(lax.rem(i, 2) == 1)
         def _():
             rs_copy(k, i).start()
 
+        @pl.when(i == ny + 2)
+        def _():
+            rs_side_copy(k).start()
+
     lag = 3
 
-    def rs_step(n, carry):
+    def side_step(n, carry):
+        @pl.when(n < chips)
+        def _():
+            rs_terms(1, n, lambda span: mm(gb[...], wg[:, span]) + mm(ub[...], wu[:, span]))
+
+        @pl.when(n >= lag)
+        def _():
+            rs_send(1, rs_join(1, n - lag))
+
+        return carry
+
+    lax.fori_loop(0, chips + lag, side_step, 0)
+
+    def down_step(n, carry):
         @pl.when(n < chips)
         def _():
             rs_terms(0, n, lambda span: mm(hid[...], wd[:, span]))
 
-        @pl.when((n >= chips) & (n < 2 * chips))
-        def _():
-            rs_terms(
-                1, n - chips, lambda span: mm(gb[...], wg[:, span]) + mm(ub[...], wu[:, span])
-            )
-
         @pl.when(n >= lag)
         def _():
-            rs_send(n - lag)
+            rs_join(0, n - lag)
 
         return carry
 
-    lax.fori_loop(0, 2 * chips + lag, rs_step, 0)
+    lax.fori_loop(0, ny, down_step, 0)
+    rs_far(1)
+    rs_relay(1)
+    lax.fori_loop(ny, chips + lag, down_step, 0)
 
     ex_ar3.wait()
     line = jnp.sum(ar3[...], axis=0)
@@ -573,6 +636,11 @@
 
     for src, dst in ((gs, gst), (us, ust), (hs, hst)):
         dst[...] = src[...].T.astype(BF16)
+    def down_sends(n, carry):
+        rs_send(0, rs_index(n))
+        return carry
+
+    lax.fori_loop(0, chips, down_sends, 0)
 
     def weight_grads(j, carry):
         span = pl.ds(pl.multiple_of(j * 2 * f_n, 2 * f_n), 2 * f_n)
@@ -583,16 +651,11 @@
         down_ref[:, span] = mm(hst[...], both_g).astype(BF16)
         return carry
 
-    lax.fori_loop(0, chips, weight_grads, 0)
+    early = chips - 3
+    lax.fori_loop(0, early, weight_grads, 0)
 
     def rs_finish(k):
-        def step(i, total):
-            remote(
-                rs_in.at[k, i], rs_in.at[k, i], rs_sem.at[k, 0, i], rs_sem.at[k, 1, i], "dp", chip_before(i) * 2 + core
-            ).wait_recv()
-            return total + rs_in[k, i].astype(F32)
-
-        total = lax.fori_loop(1, chips, step, rs_out[k, 0].astype(F32))
+        total = rs_total(k, 0, (3, 1, 4, 2))
         wide_rows = lax.dot_general(
             compact, total.astype(BF16), (((0,), (0,)), ((), ())), preferred_element_type=F32
         )
@@ -600,9 +663,10 @@
         bk_in[k, me_e] = bk_out[k, me_e]
         ex_bk[k].start()
 
-    rs_finish(0)
-
     rs_finish(1)
+    rs_far(0)
+
+    lax.fori_loop(early, chips, weight_grads, 0)
     ex_sb.wait()
     table = jnp.concatenate([sb_in[e] for e in range(ne)], axis=0)
     by_spot = mm(spread_rows.astype(F32), table, NN, HIGH)
@@ -627,43 +691,20 @@
         ex_dl.wait_for(j)
         here_dec = dec[j]
         return (
-            here_dec[0:1] * state + st[j],
-            here_dec[0:1] * slope + here_dec[1:2] * state + dl[j],
+            here_dec[0:1] * state + st[j].astype(F32),
+            here_dec[0:1] * slope + here_dec[1:2] * state + dl[j].astype(F32),
         )
 
     zero_state = jnp.zeros((n_state, f_n), F32)
     slope_in = lax.fori_loop(0, me_e, carry_slope, (zero_state, zero_state))[1]
 
-    for ex in (ex_ar1, ex_ar2, ex_ar3, ex_dec, ex_og, ex_xs, ex_sq):
-        ex.drain()
-    ex_st.drain()
-    ex_dl.drain()
-    ag_drain(rows_g, 0)
-    ag_drain(rows_u, 1)
-    for k in range(2):
-        def step(i, carry, k=k):
-            pair_copy(k, i).wait_send()
-
-            @pl.when(i > 0)
-            def _():
-                rs_copy(k, i).wait_send()
-
-            return carry
-
-        lax.fori_loop(0, chips, step, 0)
-
-    ex_bk[0].wait()
-    came = from_blocks(bk_in.at[0])
-    block_ref[...] = (
-        resid.astype(F32) + (first_m * mm(pick_at, came) + second_m * mm(pick_bt, came))
-    ).astype(BF16)
-
+    rs_relay(0)
     ex_bk[1].wait()
     moe_grad = mm(pick_at + pick_bt, from_blocks(bk_in.at[1])).T
     grad = resid_base + scale_two * moe_grad
     state_grads = [mm(c_rows * fades[h], grad, NT, HIGH) for h in range(heads)]
     state_grad = jnp.where(head_lane, state_grads[0], state_grads[1])
-    sg[me_e] = state_grad
+    sg[me_e] = state_grad.astype(BF16)
     ex_sg.start()
 
     normed_rows = normed.T
@@ -694,10 +735,31 @@
     )
     normed_grad = normed_grad + skip_f * grad
 
+    rs_finish(0)
+    for ex in (ex_ar1, ex_ar2, ex_ar3, ex_dec, ex_og, ex_xs, ex_sq):
+        ex.drain()
+    ex_st.drain()
+    ex_dl.drain()
+    ag_drain(rows_g, 0)
+    ag_drain(rows_u, 1)
+    for k in range(2):
+        def step(i, carry, k=k):
+            pair_copy(k, i).wait_send()
+
+            @pl.when((lax.rem(i, 2) == 1) | (i == 2))
+            def _():
+                rs_copy(k, i).wait_send()
+
+            return carry
+
+        lax.fori_loop(0, chips, step, 0)
+        rs_cross(k).wait_send()
+        rs_side_copy(k).wait_send()
+
     def carry_grad(n, later):
         j = ne - 1 - n
         ex_sg.wait_for(j)
-        return dec[j][0:1] * later + sg[j]
+        return dec[j][0:1] * later + sg[j].astype(F32)
 
     later = lax.fori_loop(0, ne - 1 - me_e, carry_grad, zero_state)
     normed_grad = normed_grad + tail * mm(later.T, b_rows, NN, HIGH)
@@ -705,6 +767,12 @@
     ex_ar4.start()
     ex_rout.wait()
     router_ref[...] = jnp.sum(rout[...], axis=0)
+    ex_bk[0].wait()
+    came = from_blocks(bk_in.at[0])
+    block_ref[...] = (
+        resid.astype(F32) + (first_m * mm(pick_at, came) + second_m * mm(pick_bt, came))
+    ).astype(BF16)
+
     ex_ar4.wait()
     inner_one = jnp.sum(ar4[...], axis=0)
     token_grad = (
@@ -798,14 +866,15 @@
         h(2, chips, rows, f_n),
         h(2, chips, rows, f_n),
         h(2, chips, rows, f_n),
+        h(2, rows, f_n),
         v(nd, 1, t_n),
         v(nd, 2, t_n),
         v(nd, ne, 128),
         v(nd, 1, t_n),
         v(ne, 2, f_n),
-        v(ne, n_state, f_n),
-        v(ne, n_state, f_n),
-        v(ne, n_state, f_n),
+        h(ne, n_state, f_n),
+        h(ne, n_state, f_n),
+        h(ne, n_state, f_n),
         v(ne, 1, 128),
         v(ne, ne, f_n),
         h(ne, pad, f_n),

time: 89.8 us -> 77.2 us (0.86)
  Pallas kernels: 89.1 us -> 76.5 us
    pallas_call x1, Pallas kernels: 86.1 us -> 73.5 us  [body(): pl.pallas_call(functools.partial(block_kernel, (nd, ne, t_n, f_n, d_all,...]
where the time goes in v3:
time: 77.2 us
  Pallas kernels  76.5 us (99%)
    pallas_call x1, Pallas kernels, body(): pl.pallas_call(functools.partial(block_kernel, (nd, ne, t_n, f_n, d_all,...  73.5 us
    pallas_call x1, Pallas kernels, body(): pl.pallas_call(flush_kernel, out_shape=[shape(a.shape, a.dtype) for a in...  3.01 us

profile of v3, /device:TPU:1, one launch (start us, length us, event | category | flops | bytes accessed | tf_op | source)
XLA Modules:
  0.0 77.2 jit_solution(6583121999285154519)
XLA Ops:
  0.6 73.5 %block.1 = (bf16[128,128]{1,0:T(8,128)(2,1)S(1)}, bf16[128,128]{1,0:T(8,128)(2,1)S(1)}, f32[16,128]{1,0:T(8,128)S(1)}, f32[1,128]{1,0:T(1,128)S(1)}, bf16[448,20...) custom-call(bf16[128,128]{1,0:T(8,128)(2,1)} %refs_0_.1, s32[2,128]{1,0:T(2,128)} %bitcast.26, ...), custom_call_target="tpu_custom_call" | custom-call | tf_op jit(solution)/shard_map/block/pallas_call | solution.py:901
  74.1 3.0 %flush.1 = (bf16[448,2048]{1,0:T(8,128)(2,1)}, bf16[448,2048]{1,0:T(8,128)(2,1)}, bf16[448,2048]{1,0:T(8,128)(2,1)}, bf16[128,128]{1,0:T(8,128)(2,1)}, bf16[128,...) custom-call(bf16[448,2048]{1,0:T(8,128)(2,1)S(1)} %get-tuple-element.23.refs_0_, ...), custom_call_target="tpu_custom_call" | custom-call | tf_op jit(solution)/shard_map/flush/pallas_call | solution.py:935

commit v4 on v3

--- a/solution.py
+++ b/solution.py
@@ -182,6 +182,14 @@
     bk_in,
     mt,
     spread,
+    gate_made,
+    up_made,
+    down_made,
+    cf_out,
+    cf_in,
+    diag,
+    lo_out,
+    lo_in,
     local_sem,
     ag_sem,
     pair_sem,
@@ -250,8 +258,11 @@
     ex_sq = on_expert(sq_in, 9, sq_out)
     ex_sb = on_expert(sb_in, 10, sb_out)
     ex_bk = [on_expert(bk_in.at[k], 11 + k, bk_out.at[k]) for k in range(2)]
-    ex_st, ex_dl, ex_sg = (
-        Chain("expert", me_e, ne, r, sem_e.at[k], k < 2) for k, r in enumerate((st, dl, sg))
+    ex_cf = on_expert(cf_in, 13, cf_out)
+    ex_lo = on_expert(lo_in, 14, lo_out)
+    ex_dl = on_expert(dl, 15)
+    ex_st, ex_sg = (
+        Chain("expert", me_e, ne, r, sem_e, k == 0) for k, r in enumerate((st, sg))
     )
 
     for copy in small_copies:
@@ -343,16 +354,26 @@
     )
     mixed = mixed + skip_f * normed
 
+    def ag_group(k, i):
+        return chips if k == 0 or i < ny else chips + 1 if i != ny + 2 else chips + 2
+
     def ag_send(buf, k, i, spot, peer):
         piece = buf.at[spot]
-        remote(piece, piece, ag_sem.at[k, 0, i], ag_sem.at[k, 1, i], "dp", peer * 2 + core).start()
+        remote(piece, piece, ag_sem.at[k, 0], ag_sem.at[k, i], "dp", peer * 2 + core).start()
+
+    def ag_pass(buf, k, i):
+        piece = buf.at[chip_before(i) * 2 + core]
+        remote(piece, piece, ag_sem.at[k, 0], ag_sem.at[k, ag_group(k, i)], "dp", partner).start()
 
     def ag_begin(buf, k):
         for i in (2, ny, 1, 3):
             ag_send(buf, k, i, me_d, chip_after(i))
-        remote(
-            buf.at[me_d], buf.at[me_d], ag_sem.at[k, 2, 0], ag_sem.at[k, 3, 0], "dp", partner
-        ).start()
+        ag_pass(buf, k, 0)
+
+    def ag_arrived(buf, k, i):
+        spot = chip_before(i) * 2 + core
+        remote(buf.at[spot], buf.at[spot], ag_sem.at[k, 0], ag_sem.at[k, i], "dp", spot).wait_recv()
+        return spot
 
     def ag_relay(buf, k):
         spot = ag_arrived(buf, k, ny)
@@ -363,46 +384,21 @@
         ag_send(buf, k, ny + 2, spot, chip_after(ny))
         ag_pass(buf, k, 2)
 
-    def ag_arrived(buf, k, i):
-        spot = chip_before(i) * 2 + core
-        remote(
-            buf.at[spot], buf.at[spot], ag_sem.at[k, 0, i], ag_sem.at[k, 1, i], "dp", chip_before(i) * 2 + core
-        ).wait_recv()
-        return spot
-
-    def ag_pass(buf, k, i):
-        spot = buf.at[chip_before(i) * 2 + core]
-        remote(spot, spot, ag_sem.at[k, 2, i], ag_sem.at[k, 3, i], "dp", partner).start()
-
     def ag_forward(buf, k, i):
         ag_arrived(buf, k, i)
         ag_pass(buf, k, i)
 
-    def ag_partner(buf, k, i):
-        spot = buf.at[chip_before(i) * 2 + 1 - core]
-        remote(spot, spot, ag_sem.at[k, 2, i], ag_sem.at[k, 3, i], "dp", partner).wait_recv()
-
     def ag_drain(buf, k):
-        def step(i, carry):
-            remote(
-                buf.at[me_d], buf.at[me_d], ag_sem.at[k, 0, i], ag_sem.at[k, 1, i], "dp", chip_after(i) * 2 + core
-            ).wait_send()
-            spot = buf.at[chip_before(i) * 2 + core]
-            remote(spot, spot, ag_sem.at[k, 2, i], ag_sem.at[k, 3, i], "dp", partner).wait_send()
-            return carry
-
-        remote(
-            buf.at[me_d], buf.at[me_d], ag_sem.at[k, 2, 0], ag_sem.at[k, 3, 0], "dp", partner
-        ).wait_send()
-        lax.fori_loop(1, chips, step, 0)
+        every = buf.at[pl.ds(0, 2 * chips - 1)]
+        remote(every, every, ag_sem.at[k, 0], ag_sem.at[k, 1], "dp", partner).wait_send()
 
     def ag_forwards(buf, k, turns):
         for i in turns:
             ag_forward(buf, k, i)
 
     def ag_partners(buf, k, turns):
-        for i in turns:
-            ag_partner(buf, k, i)
+        group = buf.at[pl.ds(0, len(turns))]
+        remote(group, group, ag_sem.at[k, 0], ag_sem.at[k, ag_group(k, turns[0])], "dp", partner).wait_recv()
 
     def ag_chips(buf, turns):
         places = [chip_before(i) for i in turns]
@@ -421,7 +417,6 @@
     ag_begin(rows_g, 0)
 
     ex_dec.wait()
-    ag_relay(rows_g, 0)
 
     def carry_state(j, state):
         ex_st.wait_for(j)
@@ -446,6 +441,7 @@
         axis=0,
     )
     ex_ar2.start()
+    ag_relay(rows_g, 0)
     ag_forwards(rows_g, 0, (1, 3, 5, 7, 6))
 
     ex_ar2.wait()
@@ -477,6 +473,13 @@
     weight_copies[1].wait()
     weight_copies[2].wait()
     ex_dl.start()
+    coefs = jnp.concatenate([c_rows * (fades[h] * scale_two) for h in range(heads)], axis=0)
+    by_slot = mm(coefs.astype(BF16), pick, NT)
+    cf_out[...] = jnp.zeros_like(cf_out)
+    for e in range(ne):
+        cf_out[e, :, 0:pad] = by_slot[:, e * pad : (e + 1) * pad].astype(BF16)
+    cf_in[me_e] = cf_out[me_e]
+    ex_cf.start()
     ag_relay(rows_u, 1)
     ag_forwards(rows_u, 1, (1, 3))
     take_rows((0, 1, 2, 3), True)
@@ -528,43 +531,39 @@
 
     def pair_copy(k, j):
         return remote(
-            pair_out.at[k, j], pair_in.at[k, j], pair_sem.at[k, 0, j], pair_sem.at[k, 1, j], "dp", partner
+            pair_out.at[k, j], pair_in.at[k, j], pair_sem.at[k, 0], pair_sem.at[k, 1 + j], "dp", partner
         )
 
-    def rs_copy(k, i):
+    def rs_move(k, src, i, group, peer):
         return remote(
-            rs_out.at[k, i], rs_in.at[k, i], rs_sem.at[k, 0, i], rs_sem.at[k, 1, i], "dp", chip_after(lax.rem(i, ny)) * 2 + core
+            src, rs_in.at[k, i], rs_sem.at[k, 0], rs_sem.at[k, group], "dp", peer * 2 + core
         )
 
-    def rs_arrival(k, i):
-        spot = rs_in.at[k, i]
-        return remote(spot, spot, rs_sem.at[k, 0, i], rs_sem.at[k, 1, i], "dp", partner)
-
-    def rs_side_copy(k):
-        return remote(
-            rs_out.at[k, ny + 2], rs_in.at[k, ny + 2], rs_sem.at[k, 0, ny + 2], rs_sem.at[k, 1, ny + 2], "dp", chip_after(ny) * 2 + core
-        )
+    def rs_wait(k, group, blocks):
+        span = rs_in.at[k, pl.ds(0, blocks)]
+        remote(span, span, rs_sem.at[k, 0], rs_sem.at[k, group], "dp", partner).wait_recv()
 
     def rs_far(k):
-        rs_arrival(k, ny + 2).wait_recv()
+        rs_wait(k, 2, 1)
         rs_out[k, 2] = (rs_out[k, 2].astype(F32) + rs_in[k, ny + 2].astype(F32)).astype(BF16)
-        rs_copy(k, 2).start()
-
-    def rs_cross(k):
-        return remote(
-            cross.at[k], rs_in.at[k, ny], rs_sem.at[k, 0, ny], rs_sem.at[k, 1, ny], "dp", chip_after(ny) * 2 + core
-        )
+        rs_move(k, rs_out.at[k, 2], 2, 3, chip_after(2)).start()
 
     def rs_total(k, first, turns):
         total = rs_out[k, first].astype(F32)
         for i in turns:
-            rs_arrival(k, i).wait_recv()
             total = total + rs_in[k, i].astype(F32)
         return total
 
     def rs_relay(k):
+        rs_wait(k, 1, 2)
         cross[k] = rs_total(k, ny, (ny + 3, ny + 1)).astype(BF16)
-        rs_cross(k).start()
+        rs_move(k, cross.at[k], ny, 3, chip_after(ny)).start()
+
+    def rs_drain(k):
+        span = pair_out.at[k]
+        remote(span, span, pair_sem.at[k, 0], pair_sem.at[k, 1], "dp", partner).wait_send()
+        span = rs_out.at[k, pl.ds(0, chips - 1)]
+        remote(span, span, rs_sem.at[k, 0], rs_sem.at[k, 1], "dp", partner).wait_send()
 
     def rs_index(n):
         return (1 - n // ny) * ny + lax.rem(n + 2 + n // ny, ny)
@@ -582,7 +581,7 @@
         i = rs_index(n)
         j = chip_after(i)
         remote(
-            pair_in.at[k, j], pair_in.at[k, j], pair_sem.at[k, 0, j], pair_sem.at[k, 1, j], "dp", partner
+            pair_in.at[k, j], pair_in.at[k, j], pair_sem.at[k, 0], pair_sem.at[k, 1 + j], "dp", partner
         ).wait_recv()
         rs_out[k, i] = (keep[k, j] + pair_in[k, j].astype(F32)).astype(BF16)
         return i
@@ -590,11 +589,11 @@
     def rs_send(k, i):
         @pl.when(lax.rem(i, 2) == 1)
         def _():
-            rs_copy(k, i).start()
+            rs_move(k, rs_out.at[k, i], i, 3 - i // ny * 2, chip_after(lax.rem(i, ny))).start()
 
         @pl.when(i == ny + 2)
         def _():
-            rs_side_copy(k).start()
+            rs_move(k, rs_out.at[k, i], i, 2, chip_after(ny)).start()
 
     lag = 3
 
@@ -610,22 +609,6 @@
         return carry
 
     lax.fori_loop(0, chips + lag, side_step, 0)
-
-    def down_step(n, carry):
-        @pl.when(n < chips)
-        def _():
-            rs_terms(0, n, lambda span: mm(hid[...], wd[:, span]))
-
-        @pl.when(n >= lag)
-        def _():
-            rs_join(0, n - lag)
-
-        return carry
-
-    lax.fori_loop(0, ny, down_step, 0)
-    rs_far(1)
-    rs_relay(1)
-    lax.fori_loop(ny, chips + lag, down_step, 0)
 
     ex_ar3.wait()
     line = jnp.sum(ar3[...], axis=0)
@@ -634,39 +617,29 @@
     sb_in[me_e] = sb_out[me_e]
     ex_sb.start()
 
-    for src, dst in ((gs, gst), (us, ust), (hs, hst)):
-        dst[...] = src[...].T.astype(BF16)
+    def down_step(n, carry):
+        @pl.when(n < chips)
+        def _():
+            rs_terms(0, n, lambda span: mm(hid[...], wd[:, span]))
+
+        @pl.when(n >= lag)
+        def _():
+            rs_join(0, n - lag)
+
+        return carry
+
+    lax.fori_loop(0, ny, down_step, 0)
+    rs_far(1)
+    lax.fori_loop(ny, chips - 1, down_step, 0)
+    rs_relay(1)
+    lax.fori_loop(chips - 1, chips + lag, down_step, 0)
+
     def down_sends(n, carry):
         rs_send(0, rs_index(n))
         return carry
 
     lax.fori_loop(0, chips, down_sends, 0)
 
-    def weight_grads(j, carry):
-        span = pl.ds(pl.multiple_of(j * 2 * f_n, 2 * f_n), 2 * f_n)
-        both_u = jnp.concatenate([rows_u[2 * j], rows_u[2 * j + 1]], axis=1)
-        both_g = jnp.concatenate([rows_g[2 * j], rows_g[2 * j + 1]], axis=1)
-        gate_ref[:, span] = mm(gst[...], both_u).astype(BF16)
-        up_ref[:, span] = mm(ust[...], both_u).astype(BF16)
-        down_ref[:, span] = mm(hst[...], both_g).astype(BF16)
-        return carry
-
-    early = chips - 3
-    lax.fori_loop(0, early, weight_grads, 0)
-
-    def rs_finish(k):
-        total = rs_total(k, 0, (3, 1, 4, 2))
-        wide_rows = lax.dot_general(
-            compact, total.astype(BF16), (((0,), (0,)), ((), ())), preferred_element_type=F32
-        )
-        to_blocks(bk_out.at[k], wide_rows)
-        bk_in[k, me_e] = bk_out[k, me_e]
-        ex_bk[k].start()
-
-    rs_finish(1)
-    rs_far(0)
-
-    lax.fori_loop(early, chips, weight_grads, 0)
     ex_sb.wait()
     table = jnp.concatenate([sb_in[e] for e in range(ne)], axis=0)
     by_spot = mm(spread_rows.astype(F32), table, NN, HIGH)
@@ -685,10 +658,58 @@
     )
     first_m = jnp.broadcast_to(first_w, (f_n, t_n)).T
     second_m = jnp.broadcast_to(second_w, (f_n, t_n)).T
-
+    base_grads = [mm(c_rows * fades[h], resid_base, NT, HIGH) for h in range(heads)]
+    sg[me_e] = jnp.where(head_lane, base_grads[0], base_grads[1]).astype(BF16)
+    ex_sg.start()
+
+    ex_cf.wait()
+    width = heads * n_state
+    taken = jnp.concatenate([cf_in[b].astype(F32) for b in range(ne)], axis=0).astype(BF16)
+    repeat = (iota((128, spots), 0) == iota((128, spots), 1) % pad).astype(BF16)
+    own_block = iota((ne * width, spots), 0) // width == iota((ne * width, spots), 1) // pad
+    diag[...] = jnp.where(own_block, mm(taken, repeat), 0.0).astype(BF16)
+    for src, dst in ((gs, gst), (us, ust), (hs, hst)):
+        dst[...] = src[...].T.astype(BF16)
+    def rs_finish(k):
+        rs_wait(k, 3, 4)
+        total = rs_total(k, 0, (3, 1, ny, 2))
+        wide_rows = lax.dot_general(
+            compact, total.astype(BF16), (((0,), (0,)), ((), ())), preferred_element_type=F32
+        )
+        to_blocks(bk_out.at[k], wide_rows)
+        bk_in[k, me_e] = bk_out[k, me_e]
+        ex_bk[k].start()
+        return wide_rows
+
+    back_rows = rs_finish(1)
+    shares = mm(diag[...], back_rows.astype(BF16))
+    later = jnp.zeros((n_state, f_n), F32)
+    lo_out[ne - 1] = later.astype(BF16)
+    for b in range(ne - 1, 0, -1):
+        low = shares[b * width : b * width + n_state]
+        high = shares[b * width + n_state : (b + 1) * width]
+        later = jnp.where(head_lane, low, high) + dec[b][0:1] * later
+        lo_out[b - 1] = later.astype(BF16)
+    lo_in[me_e] = lo_out[me_e]
+    ex_lo.start()
+
+    rs_far(0)
+
+    def weight_grads(j, carry):
+        span = pl.ds(pl.multiple_of(j * 2 * f_n, 2 * f_n), 2 * f_n)
+        both_u = jnp.concatenate([rows_u[2 * j], rows_u[2 * j + 1]], axis=1)
+        both_g = jnp.concatenate([rows_g[2 * j], rows_g[2 * j + 1]], axis=1)
+        gate_made[:, span] = mm(gst[...], both_u).astype(BF16)
+        up_made[:, span] = mm(ust[...], both_u).astype(BF16)
+        down_made[:, span] = mm(hst[...], both_g).astype(BF16)
+        return carry
+
+    early = chips - 3
+    lax.fori_loop(0, early, weight_grads, 0)
+    rs_relay(0)
+    lax.fori_loop(early, chips, weight_grads, 0)
     def carry_slope(j, both):
         state, slope = both
-        ex_dl.wait_for(j)
         here_dec = dec[j]
         return (
             here_dec[0:1] * state + st[j].astype(F32),
@@ -696,16 +717,15 @@
         )
 
     zero_state = jnp.zeros((n_state, f_n), F32)
+    ex_dl.wait()
     slope_in = lax.fori_loop(0, me_e, carry_slope, (zero_state, zero_state))[1]
 
-    rs_relay(0)
+    rs_finish(0)
     ex_bk[1].wait()
     moe_grad = mm(pick_at + pick_bt, from_blocks(bk_in.at[1])).T
     grad = resid_base + scale_two * moe_grad
     state_grads = [mm(c_rows * fades[h], grad, NT, HIGH) for h in range(heads)]
     state_grad = jnp.where(head_lane, state_grads[0], state_grads[1])
-    sg[me_e] = state_grad.astype(BF16)
-    ex_sg.start()
 
     normed_rows = normed.T
     cum_f = jnp.where(head_row, cum[0:1], cum[1:2])
@@ -735,7 +755,23 @@
     )
     normed_grad = normed_grad + skip_f * grad
 
-    rs_finish(0)
+    def carry_grad(n, later):
+        j = ne - 1 - n
+        ex_sg.wait_for(j)
+        return dec[j][0:1] * later + sg[j].astype(F32)
+
+    ex_lo.wait()
+    later = lax.fori_loop(0, ne - 1 - me_e, carry_grad, zero_state)
+    later = later + jnp.sum(lo_in[...].astype(F32), axis=0)
+    normed_grad = normed_grad + tail * mm(later.T, b_rows, NN, HIGH)
+    ar4[me_d] = jnp.sum(normed_grad * x_t, axis=0, keepdims=True)
+    ex_ar4.start()
+    grad_copies = [
+        pltpu.make_async_copy(src, dst, local_sem.at[k])
+        for k, (src, dst) in enumerate(((gate_made, gate_ref), (up_made, up_ref), (down_made, down_ref)))
+    ]
+    for copy in grad_copies:
+        copy.start()
     for ex in (ex_ar1, ex_ar2, ex_ar3, ex_dec, ex_og, ex_xs, ex_sq):
         ex.drain()
     ex_st.drain()
@@ -743,28 +779,8 @@
     ag_drain(rows_g, 0)
     ag_drain(rows_u, 1)
     for k in range(2):
-        def step(i, carry, k=k):
-            pair_copy(k, i).wait_send()
-
-            @pl.when((lax.rem(i, 2) == 1) | (i == 2))
-            def _():
-                rs_copy(k, i).wait_send()
-
-            return carry
-
-        lax.fori_loop(0, chips, step, 0)
-        rs_cross(k).wait_send()
-        rs_side_copy(k).wait_send()
-
-    def carry_grad(n, later):
-        j = ne - 1 - n
-        ex_sg.wait_for(j)
-        return dec[j][0:1] * later + sg[j].astype(F32)
-
-    later = lax.fori_loop(0, ne - 1 - me_e, carry_grad, zero_state)
-    normed_grad = normed_grad + tail * mm(later.T, b_rows, NN, HIGH)
-    ar4[me_d] = jnp.sum(normed_grad * x_t, axis=0, keepdims=True)
-    ex_ar4.start()
+        rs_drain(k)
+
     ex_rout.wait()
     router_ref[...] = jnp.sum(rout[...], axis=0)
     ex_bk[0].wait()
@@ -782,9 +798,13 @@
     ex_tot.wait()
     small_ref[...] = jnp.sum(tot[...], axis=0)
 
+    for copy in grad_copies:
+        copy.wait()
     for ex in (ex_ar4, ex_tot, ex_rout, ex_sb, *ex_bk):
         ex.drain()
     ex_sg.drain()
+    ex_cf.drain()
+    ex_lo.drain()
 
 
 def flush_kernel(*refs):
@@ -889,12 +909,20 @@
         h(2, ne, pad, f_n),
         v(heads, t_n, t_n),
         v(heads, t_n, t_n),
+        h(units, d_all),
+        h(units, d_all),
+        h(units, d_all),
+        h(ne, heads * n_state, 128),
+        h(ne, heads * n_state, 128),
+        h(ne * heads * n_state, ne * pad),
+        h(ne, n_state, f_n),
+        h(ne, n_state, f_n),
         pltpu.SemaphoreType.DMA((12,)),
-        pltpu.SemaphoreType.DMA((2, 4, chips)),
-        pltpu.SemaphoreType.DMA((2, 2, chips)),
-        pltpu.SemaphoreType.DMA((2, 2, chips)),
-        pltpu.SemaphoreType.DMA((13, 2)),
-        pltpu.SemaphoreType.DMA((3, 2, ne)),
+        pltpu.SemaphoreType.DMA((2, chips + 3)),
+        pltpu.SemaphoreType.DMA((2, 1 + chips)),
+        pltpu.SemaphoreType.DMA((2, 4)),
+        pltpu.SemaphoreType.DMA((16, 2)),
+        pltpu.SemaphoreType.DMA((2, ne)),
     ]
     grad_shape = h(units, d_all)
     token_shape = h(t_n, f_n)
@@ -910,7 +938,7 @@
             grad_shape,
         ],
         in_specs=[hbm] * 12,
-        out_specs=[vmem] * 7,
+        out_specs=[vmem] * 4 + [anywhere] * 3,
         scratch_shapes=scratch,
         compiler_params=pltpu.CompilerParams(
             collective_id=0, has_side_effects=True, vmem_limit_bytes=61400000

time: 77.2 us -> 73.4 us (0.951)
  Pallas kernels: 76.5 us -> 72.7 us
    pallas_call x1, Pallas kernels: 73.5 us -> 69.6 us  [body(): pl.pallas_call(functools.partial(block_kernel, (nd, ne, t_n, f_n, d_all,...]
where the time goes in v4:
time: 73.4 us; the launch traced here: 73.3 us
  Pallas kernels  72.7 us (99%)
    pallas_call x1, Pallas kernels, body(): pl.pallas_call(functools.partial(block_kernel, (nd, ne, t_n, f_n, d_all,...  69.6 us
    pallas_call x1, Pallas kernels, body(): pl.pallas_call(flush_kernel, out_shape=[shape(a.shape, a.dtype) for a in...  3.01 us

profile of v4, /device:TPU:1, one launch (start us, length us, event | category | flops | bytes accessed | tf_op | source)
XLA Modules:
  0.0 73.3 jit_solution(10689379444448822050)
XLA Ops:
  0.6 69.6 %block.1 = (bf16[128,128]{1,0:T(8,128)(2,1)S(1)}, bf16[128,128]{1,0:T(8,128)(2,1)S(1)}, f32[16,128]{1,0:T(8,128)S(1)}, f32[1,128]{1,0:T(1,128)S(1)}, bf16[448,20...) custom-call(bf16[128,128]{1,0:T(8,128)(2,1)} %refs_0_.1, s32[2,128]{1,0:T(2,128)} %bitcast.26, ...), custom_call_target="tpu_custom_call" | custom-call | tf_op jit(solution)/shard_map/block/pallas_call | solution.py:929
  70.3 3.0 %flush.1 = (bf16[448,2048]{1,0:T(8,128)(2,1)}, bf16[448,2048]{1,0:T(8,128)(2,1)}, bf16[448,2048]{1,0:T(8,128)(2,1)}, bf16[128,128]{1,0:T(8,128)(2,1)}, bf16[128,...) custom-call(bf16[448,2048]{1,0:T(8,128)(2,1)S(1)} %get-tuple-element.23.refs_0_, ...), custom_call_target="tpu_custom_call" | custom-call | tf_op jit(solution)/shard_map/flush/pallas_call | solution.py:963

commit v5 on v4

--- a/solution.py
+++ b/solution.py
@@ -146,9 +146,6 @@
     hid,
     gb,
     ub,
-    gs,
-    us,
-    hs,
     gst,
     ust,
     hst,
@@ -510,9 +507,6 @@
         hid[span] = hidden.astype(BF16)
         gb[span] = gate_back.astype(BF16)
         ub[span] = up_back.astype(BF16)
-        gs[span] = gate_back * scale
-        us[span] = up_back * scale
-        hs[span] = hidden * weight
         pair_sum = jnp.sum(hidden * grad_in, axis=1, keepdims=True)
         inner_sum = jnp.sum(gate_back * gate_in + up_back * up_in, axis=1, keepdims=True)
         lane = iota((part, 128), 1)
@@ -668,8 +662,6 @@
     repeat = (iota((128, spots), 0) == iota((128, spots), 1) % pad).astype(BF16)
     own_block = iota((ne * width, spots), 0) // width == iota((ne * width, spots), 1) // pad
     diag[...] = jnp.where(own_block, mm(taken, repeat), 0.0).astype(BF16)
-    for src, dst in ((gs, gst), (us, ust), (hs, hst)):
-        dst[...] = src[...].T.astype(BF16)
     def rs_finish(k):
         rs_wait(k, 3, 4)
         total = rs_total(k, 0, (3, 1, ny, 2))
@@ -695,6 +687,10 @@
 
     rs_far(0)
 
+    rs_relay(0)
+    for src, dst, k in ((gb, gst, 0), (ub, ust, 0), (hid, hst, 1)):
+        dst[...] = (src[...].astype(F32) * cols[k]).T.astype(BF16)
+
     def weight_grads(j, carry):
         span = pl.ds(pl.multiple_of(j * 2 * f_n, 2 * f_n), 2 * f_n)
         both_u = jnp.concatenate([rows_u[2 * j], rows_u[2 * j + 1]], axis=1)
@@ -706,7 +702,6 @@
 
     early = chips - 3
     lax.fori_loop(0, early, weight_grads, 0)
-    rs_relay(0)
     lax.fori_loop(early, chips, weight_grads, 0)
     def carry_slope(j, both):
         state, slope = both
@@ -719,35 +714,29 @@
     zero_state = jnp.zeros((n_state, f_n), F32)
     ex_dl.wait()
     slope_in = lax.fori_loop(0, me_e, carry_slope, (zero_state, zero_state))[1]
+    slope_col = slope_in.T
+    cum_f = jnp.where(head_row, cum[0:1], cum[1:2])
+    by_rate = jnp.concatenate(
+        [
+            mm(slope_col[h * hp : (h + 1) * hp], c_rows * fades[h], NN, HIGH)
+            - mm(normed[h * hp : (h + 1) * hp], mt[h] * spread[h], NN, HIGH)
+            for h in range(heads)
+        ],
+        axis=0,
+    )
+    by_rate = by_rate - cum_f * from_state
 
     rs_finish(0)
     ex_bk[1].wait()
     moe_grad = mm(pick_at + pick_bt, from_blocks(bk_in.at[1])).T
     grad = resid_base + scale_two * moe_grad
-    state_grads = [mm(c_rows * fades[h], grad, NT, HIGH) for h in range(heads)]
-    state_grad = jnp.where(head_lane, state_grads[0], state_grads[1])
-
-    normed_rows = normed.T
-    cum_f = jnp.where(head_row, cum[0:1], cum[1:2])
-    rate_row = jnp.sum(state_grad * slope_in, axis=0, keepdims=True)
-    state_part = grad * from_state * cum_f
-    skip_part = grad * normed
     lane_s = iota((1, 128), 1)
     small = jnp.zeros((1, 128), F32)
-    for h in range(heads):
-        mine = head_row if h == 0 else jnp.logical_not(head_row)
-        mine_lane = head_lane if h == 0 else jnp.logical_not(head_lane)
-        pair_grad = mm(normed_rows, jnp.where(mine, grad, 0.0), NN, HIGH)
-        table_part = pair_grad * mt[h] * spread[h]
-        rows_h = slice(h * hp, (h + 1) * hp)
-        rate_h = (
-            jnp.sum(jnp.where(mine_lane, rate_row, 0.0), axis=1, keepdims=True)
-            - jnp.sum(jnp.sum(table_part, axis=0, keepdims=True), axis=1, keepdims=True)
-            - jnp.sum(jnp.sum(state_part[rows_h], axis=0, keepdims=True), axis=1, keepdims=True)
-        )
-        skip_h = jnp.sum(jnp.sum(skip_part[rows_h], axis=0, keepdims=True), axis=1, keepdims=True)
-        small = small + jnp.where(lane_s == h, rate_h, 0.0)
-        small = small + jnp.where(lane_s == heads + h, skip_h, 0.0)
+    for k, part in enumerate((grad * by_rate, grad * normed)):
+        for h in range(heads):
+            total = jnp.sum(part[h * hp : (h + 1) * hp], axis=0, keepdims=True)
+            total = jnp.sum(total, axis=1, keepdims=True)
+            small = small + jnp.where(lane_s == k * heads + h, total, 0.0)
     tot[me_e] = small
     ex_tot.start()
     normed_grad = jnp.concatenate(
@@ -873,9 +862,6 @@
         h(rows, units),
         h(rows, units),
         h(rows, units),
-        v(rows, units),
-        v(rows, units),
-        v(rows, units),
         h(units, rows),
         h(units, rows),
         h(units, rows),

time: 73.4 us -> 73.6 us (level)
  no operation moved by 1% of the time
where the time goes in v5:
time: 73.6 us; the launch traced here: 73.5 us
  Pallas kernels  72.8 us (99%)
    pallas_call x1, Pallas kernels, body(): pl.pallas_call(functools.partial(block_kernel, (nd, ne, t_n, f_n, d_all,...  69.8 us
    pallas_call x1, Pallas kernels, body(): pl.pallas_call(flush_kernel, out_shape=[shape(a.shape, a.dtype) for a in...  3.01 us

profile of v5, /device:TPU:1, one launch (start us, length us, event | category | flops | bytes accessed | tf_op | source)
XLA Modules:
  0.0 73.5 jit_solution(2472006014964423841)
XLA Ops:
  0.6 69.8 %block.1 = (bf16[128,128]{1,0:T(8,128)(2,1)S(1)}, bf16[128,128]{1,0:T(8,128)(2,1)S(1)}, f32[16,128]{1,0:T(8,128)S(1)}, f32[1,128]{1,0:T(1,128)S(1)}, bf16[448,20...) custom-call(bf16[128,128]{1,0:T(8,128)(2,1)} %refs_0_.1, s32[2,128]{1,0:T(2,128)} %bitcast.26, ...), custom_call_target="tpu_custom_call" | custom-call | tf_op jit(solution)/shard_map/block/pallas_call | solution.py:915
  70.5 3.0 %flush.1 = (bf16[448,2048]{1,0:T(8,128)(2,1)}, bf16[448,2048]{1,0:T(8,128)(2,1)}, bf16[448,2048]{1,0:T(8,128)(2,1)}, bf16[128,128]{1,0:T(8,128)(2,1)}, bf16[128,...) custom-call(bf16[448,2048]{1,0:T(8,128)(2,1)S(1)} %get-tuple-element.23.refs_0_, ...), custom_call_target="tpu_custom_call" | custom-call | tf_op jit(solution)/shard_map/flush/pallas_call | solution.py:949

commit v6 on v5

--- a/solution.py
+++ b/solution.py
@@ -333,6 +333,10 @@
     compact = (
         ((spot_q // pad) * cap + spot_q % pad == iota((rows, spots), 0)) & (spot_q % pad < cap)
     ).astype(BF16)
+    spot_qt = iota((spots, rows), 0)
+    compact_t = (
+        ((spot_qt // pad) * cap + spot_qt % pad == iota((spots, rows), 1)) & (spot_qt % pad < cap)
+    ).astype(BF16)
     of_block_r, of_block_b = iota((rows, ne), 0), iota((rows, ne), 1) * cap
     of_block = ((of_block_r >= of_block_b) & (of_block_r < of_block_b + cap)).astype(F32)
     lane_r = iota((rows, 128), 0)
@@ -343,7 +347,7 @@
     ex_ar1.wait()
     scale_one = lax.rsqrt(jnp.sum(ar1[...], axis=0) / d_all + EPSILON)
     normed = x_t * scale_one
-    st[me_e] = mm(b_rows, normed * tail, NT, HIGH).astype(BF16)
+    st[me_e] = mm(b_rows.astype(BF16), (normed * tail).astype(BF16), NT).astype(BF16)
     ex_st.start()
     dl[me_e] = mm(b_rows, normed * tail * reach, NT, HIGH).astype(BF16)
     mixed = jnp.concatenate(
@@ -420,9 +424,12 @@
         return dec[j][0:1] * state + st[j].astype(F32)
 
     state_in = lax.fori_loop(0, me_e, carry_state, jnp.zeros((n_state, f_n), F32))
-    state_col = state_in.T
+    state_col = state_in.T.astype(BF16)
     from_state = jnp.concatenate(
-        [mm(state_col[h * hp : (h + 1) * hp], c_rows * fades[h], NN, HIGH) for h in range(heads)],
+        [
+            mm(state_col[h * hp : (h + 1) * hp], (c_rows * fades[h]).astype(BF16))
+            for h in range(heads)
+        ],
         axis=0,
     )
     resid_t = (x_t + (mixed + from_state)).astype(BF16).astype(F32)
@@ -665,9 +672,7 @@
     def rs_finish(k):
         rs_wait(k, 3, 4)
         total = rs_total(k, 0, (3, 1, ny, 2))
-        wide_rows = lax.dot_general(
-            compact, total.astype(BF16), (((0,), (0,)), ((), ())), preferred_element_type=F32
-        )
+        wide_rows = mm(compact_t, total.astype(BF16))
         to_blocks(bk_out.at[k], wide_rows)
         bk_in[k, me_e] = bk_out[k, me_e]
         ex_bk[k].start()
@@ -752,7 +757,7 @@
     ex_lo.wait()
     later = lax.fori_loop(0, ne - 1 - me_e, carry_grad, zero_state)
     later = later + jnp.sum(lo_in[...].astype(F32), axis=0)
-    normed_grad = normed_grad + tail * mm(later.T, b_rows, NN, HIGH)
+    normed_grad = normed_grad + tail * mm(later.T.astype(BF16), b_rows.astype(BF16))
     ar4[me_d] = jnp.sum(normed_grad * x_t, axis=0, keepdims=True)
     ex_ar4.start()
     grad_copies = [

time: 73.6 us -> 72.9 us (level)
  no operation moved by 1% of the time
where the time goes in v6:
time: 72.9 us; the launch traced here: 72.8 us
  Pallas kernels  72.2 us (99%)
    pallas_call x1, Pallas kernels, body(): pl.pallas_call(functools.partial(block_kernel, (nd, ne, t_n, f_n, d_all,...  69.2 us
    pallas_call x1, Pallas kernels, body(): pl.pallas_call(flush_kernel, out_shape=[shape(a.shape, a.dtype) for a in...  3.01 us

profile of v6, /device:TPU:1, one launch (start us, length us, event | category | flops | bytes accessed | tf_op | source)
XLA Modules:
  0.0 72.8 jit_solution(2616353212643752415)
XLA Ops:
  0.6 69.2 %block.1 = (bf16[128,128]{1,0:T(8,128)(2,1)S(1)}, bf16[128,128]{1,0:T(8,128)(2,1)S(1)}, f32[16,128]{1,0:T(8,128)S(1)}, f32[1,128]{1,0:T(1,128)S(1)}, bf16[448,20...) custom-call(bf16[128,128]{1,0:T(8,128)(2,1)} %refs_0_.1, s32[2,128]{1,0:T(2,128)} %bitcast.26, ...), custom_call_target="tpu_custom_call" | custom-call | tf_op jit(solution)/shard_map/block/pallas_call | solution.py:920
  69.8 3.0 %flush.1 = (bf16[448,2048]{1,0:T(8,128)(2,1)}, bf16[448,2048]{1,0:T(8,128)(2,1)}, bf16[448,2048]{1,0:T(8,128)(2,1)}, bf16[128,128]{1,0:T(8,128)(2,1)}, bf16[128,...) custom-call(bf16[448,2048]{1,0:T(8,128)(2,1)S(1)} %get-tuple-element.23.refs_0_, ...), custom_call_target="tpu_custom_call" | custom-call | tf_op jit(solution)/shard_map/flush/pallas_call | solution.py:954
